TPU v7x, 32 devices: a whole 2x2x4 slice. The times are simulated.
32 devices in a mesh: angle: 4 (over z), pos: 8 (over y, x, core).
Axes of the slice: x: 2, y: 2, z: 4, core: 2. Of those that a mesh axis runs over, the one named last changes fastest.
Arguments:
- amplitude: float32 [4, 32, 128, 128], P('angle', 'pos'), may hold values from 0 to 2.5
- offsets: int32 [4, 32, 2], P('angle', 'pos'), may hold values from 0 to 896, as said below
- probe_field: float32 [2, 128, 128], replicated, may hold values from -5 to 5
- object_field: float32 [4, 2, 1024, 1024], P('angle', None, 'pos'), may hold values from -5 to 5
- interp_index: int32 [4, 2, 1024], replicated, may hold values from 0 to 1022
- interp_weight: float32 [4, 2, 1024], replicated, may hold values from 0 to 1
Outputs:
- new_object: float32 [4, 2, 1024, 1024], P('angle', None, 'pos')
- new_probe: float32 [2, 128, 128], replicated
- recon: float32 [8, 128, 2, 1024], P('pos', 'angle')
Inputs may be any that keep to these rules, and one draw needn't show every extreme that they name: For position j, offsets[a, j, 0] = max(0, min(896, (j // 4) * 128 - 128 // 2 + u)) with 0 <= u < 128; offsets[a, j, 1] lies in 0 to 896.
All inputs are finite; a program needn't handle non-finite values.
Results may differ from a plain program's by a relative error of at most 0.00007.
Values sent between devices are 32-bit elements; how exact they have to be, the bound alone decides.
A program may use at most 64 MiB of HBM per device.

v0:
```python
import functools
import math

import jax
import jax.numpy as jnp
import numpy as np
from jax import lax
from jax.experimental import pallas as pl
from jax.experimental.pallas import tpu as pltpu
from jax.sharding import PartitionSpec as P

MESH = pl.DeviceIdType.MESH
VMEM = pltpu.VMEM
BIG = 60 * 1024 * 1024


def split_const(table):
    high = jnp.asarray(table, jnp.float32).astype(jnp.bfloat16)
    low = (jnp.asarray(table, jnp.float32) - high.astype(jnp.float32)).astype(jnp.bfloat16)
    return high, low


def dft_blocks(length):
    ramp = np.arange(length)
    theta = (ramp[:, None] * ramp[None, :] % length) * (2.0 * math.pi / length)
    real = np.cos(theta) / math.sqrt(length)
    imag = -np.sin(theta) / math.sqrt(length)
    left = np.block([[real, -imag], [imag, real]])
    right = np.block([[real, imag], [-imag, real]])
    return np.asarray(left, np.float32), np.asarray(right, np.float32)


def halves(value):
    high = value.astype(jnp.bfloat16)
    return high, (value - high.astype(jnp.float32)).astype(jnp.bfloat16)


def mm(a, b):
    return jnp.dot(a, b, preferred_element_type=jnp.float32)


def left3(table_high, table_low, value):
    high, low = halves(value)
    return mm(table_high, high) + mm(table_high, low) + mm(table_low, high)


def right3(value, table_high, table_low):
    high, low = halves(value)
    return mm(high, table_high) + mm(low, table_high) + mm(high, table_low)


def remote(src, dst, send, recv, axis, target):
    return pltpu.make_async_remote_copy(
        src_ref=src, dst_ref=dst, send_sem=send, recv_sem=recv,
        device_id={axis: target}, device_id_type=MESH,
    )


def patch_kernel(n_pos, where_at, obj, offs, index, amp, probe, ah, al, bh, bl,
                 grad, from_above, from_below, offs_near, partial, onehot,
                 ext, table, numden, rs,
                 local_sem, table_sem, send_sem, recv_sem, rs_send, rs_recv):
    me = lax.axis_index("pos")
    up, down = lax.rem(me + n_pos - 1, n_pos), lax.rem(me + 1, n_pos)
    band = obj.shape[2]
    width = obj.shape[3]
    patch = probe.shape[1]
    half = patch // 2
    count = amp.shape[0]
    inner = pltpu.make_async_copy(obj.at[0], ext.at[:, pl.ds(half, band), :], local_sem.at[0])
    inner.start()
    barrier = pltpu.get_barrier_semaphore()
    pos_peers = [lax.rem(me + d, n_pos) for d in range(1, n_pos)]
    for target in pos_peers:
        pl.semaphore_signal(barrier, inc=1, device_id={"pos": target}, device_id_type=MESH)
    pl.semaphore_wait(barrier, n_pos - 1)
    first = [
        remote(obj.at[0, :, pl.ds(band - half, half), :], ext.at[:, pl.ds(0, half), :],
               send_sem.at[0], recv_sem.at[0], "pos", down),
        remote(obj.at[0, :, pl.ds(0, half), :], ext.at[:, pl.ds(half + band, half), :],
               send_sem.at[1], recv_sem.at[1], "pos", up),
        remote(offs, offs_near.at[0], send_sem.at[2], recv_sem.at[2], "pos", down),
        remote(offs, offs_near.at[1], send_sem.at[3], recv_sem.at[3], "pos", up),
    ]
    for copy in first:
        copy.start()
    p_re, p_im = probe[0], probe[1]
    wide_at = lax.broadcasted_iota(jnp.int32, (width, count * patch), 0)
    pick_cols = (wide_at == where_at[0:1, :]).astype(jnp.bfloat16)
    tall_at = lax.broadcasted_iota(jnp.int32, (patch, band + patch), 1)

    def choose(spans):
        parts = []
        for c in range(2):
            split = [halves(ext[c, span, :]) for span in spans]
            parts += [piece[0] for piece in split] + [piece[1] for piece in split]
        return mm(jnp.concatenate(parts, axis=0), pick_cols).astype(jnp.bfloat16)

    inner.wait()
    inside = choose((slice(half, half + band),))
    chunk = table.shape[2]
    per_row = width // chunk
    zwin = index.shape[1]
    steps = onehot.shape[0]
    bins = lax.broadcasted_iota(jnp.int32, (width, chunk), 0)

    def shipped(step, slot):
        return pltpu.make_async_copy(table.at[slot], onehot.at[step], table_sem.at[slot])

    def build(step, slot):
        a = step // (zwin * per_row)
        z = lax.rem(step // per_row, zwin)
        lanes = pl.ds(pl.multiple_of(lax.rem(step, per_row) * chunk, chunk), chunk)
        hit = bins == index[a, pl.ds(z, 1), lanes]
        table[slot] = jnp.where(hit, 1.0, 0.0).astype(jnp.bfloat16)
        shipped(step, slot).start()

    def build_pair(pair, carry):
        for slot in range(2):
            shipped(2 * pair + slot - 2, slot).wait()
            build(2 * pair + slot, slot)
        return carry

    for slot in range(2):
        build(jnp.int32(slot), slot)
    lax.fori_loop(1, steps // 2, build_pair, 0)
    for copy in first:
        copy.wait()
    outer = choose((slice(0, half), slice(half + band, patch + band)))
    n_re = jnp.zeros((patch, patch), jnp.float32)
    n_im = n_re
    den = n_re
    second = []
    size = 2 if count % 2 == 0 else count
    for g in range(count // size):
        group = range(g * size, (g + 1) * size)
        q_re, q_im, w_re, w_im = [], [], [], []
        for j in group:
            row_at = jnp.broadcast_to(where_at[1:2, j * patch:(j + 1) * patch], (patch, patch))
            row_at = jnp.transpose(row_at)[:, :1]
            pick_rows = (tall_at == row_at).astype(jnp.bfloat16)
            parts = []
            for k in range(4):
                parts += [outer[k * patch:k * patch + half, j * patch:(j + 1) * patch],
                          inside[k * band:(k + 1) * band, j * patch:(j + 1) * patch],
                          outer[k * patch + half:(k + 1) * patch, j * patch:(j + 1) * patch]]
            lines = [jnp.concatenate(parts[3 * k:3 * k + 3], axis=0) for k in range(4)]
            got = mm(pick_rows, jnp.concatenate(lines, axis=1))
            re = got[:, :patch] + got[:, patch:2 * patch]
            im = got[:, 2 * patch:3 * patch] + got[:, 3 * patch:]
            q_re.append(re)
            q_im.append(im)
            w_re.append(p_re * re - p_im * im)
            w_im.append(p_re * im + p_im * re)
        psi = jnp.concatenate([jnp.concatenate(w_re, axis=1), jnp.concatenate(w_im, axis=1)], axis=0)
        mid = left3(ah[...], al[...], psi)
        cells = [slice(n * patch, (n + 1) * patch) for n in range(size)]
        rows = [jnp.concatenate([mid[:patch, cell], mid[patch:, cell]], axis=1) for cell in cells]
        spec = right3(jnp.concatenate(rows, axis=0), bh[...], bl[...])
        fixed = []
        for j, cell in zip(group, cells):
            s_re = spec[cell, :patch]
            s_im = spec[cell, patch:]
            factor = amp[j] / jnp.maximum(jnp.sqrt(s_re * s_re + s_im * s_im), 0.5)
            fixed.append(jnp.concatenate([factor * s_re, factor * s_im], axis=1))
        back = right3(jnp.concatenate(fixed, axis=0), ah[...], al[...])
        wide_re = jnp.concatenate([back[cell, :patch] for cell in cells], axis=1)
        wide_im = jnp.concatenate([back[cell, patch:] for cell in cells], axis=1)
        diff = left3(bh[...], bl[...], jnp.concatenate([wide_re, wide_im], axis=0))
        diff = diff - psi
        for n, j in enumerate(group):
            d_re, d_im = diff[:patch, cells[n]], diff[patch:, cells[n]]
            g_re = p_re * d_re + p_im * d_im
            g_im = p_re * d_im - p_im * d_re
            for h in range(2):
                grad[h, j, 0] = g_re[h * half:(h + 1) * half]
                grad[h, j, 1] = g_im[h * half:(h + 1) * half]
            n_re = n_re + (q_re[n] * d_re + q_im[n] * d_im)
            n_im = n_im + (q_re[n] * d_im - q_im[n] * d_re)
            den = den + (q_re[n] * q_re[n] + q_im[n] * q_im[n])
        if g == count // size - 1:
            numden[0] = n_re
            numden[1] = n_im
            numden[2] = den
        span = pl.ds(g * size, size)
        sems = [4 + 2 * g, 5 + 2 * g]
        pair = [
            remote(grad.at[1, span], from_above.at[span], send_sem.at[sems[0]],
                   recv_sem.at[sems[0]], "pos", down),
            remote(grad.at[0, span], from_below.at[span], send_sem.at[sems[1]],
                   recv_sem.at[sems[1]], "pos", up),
        ]
        for copy in pair:
            copy.start()
        second += pair
    pr = patch // n_pos
    scatter = [
        remote(numden.at[:, pl.ds(pl.multiple_of(peer * pr, 8), pr), :], rs.at[d],
               rs_send.at[d], rs_recv.at[d], "pos", peer)
        for d, peer in enumerate(pos_peers)
    ]
    for copy in scatter:
        copy.start()
    for slot in range(2):
        shipped(steps - 2 + slot, slot).wait()
    for copy in scatter:
        copy.wait()
    part = numden[:, pl.ds(pl.multiple_of(me * pr, 8), pr), :]
    for d in range(n_pos - 1):
        part = part + rs[d]
    partial[...] = part
    for copy in second:
        copy.wait()


def merge_kernel(count, start_ref, own_ref, near_ref, obj, probe, grad, from_above, from_below,
                 out, acc):
    band = obj.shape[2]
    width = obj.shape[3]
    patch = probe.shape[1]
    half = patch // 2
    start = start_ref[0]
    acc[...] = jnp.zeros_like(acc)
    power = probe[0] * probe[0] + probe[1] * probe[1]
    last = acc.shape[1] - 8

    def place(planes, row, col):
        height = planes[0].shape[0]
        tile = jnp.minimum(col // 128, width // 128 - 2)
        base = pl.multiple_of(tile * 128, 128)
        shift = col - base
        top = pl.multiple_of(row // 8 * 8, 8)
        drop = row - top
        for c in range(3):
            tall = jnp.concatenate([planes[c], jnp.zeros((8, patch), jnp.float32)], axis=0)
            tall = pltpu.roll(tall, drop, 0)
            wide = jnp.concatenate([tall, jnp.zeros((height + 8, 128), jnp.float32)], axis=1)
            wide = pltpu.roll(wide, shift, 1)
            spot = (c, pl.ds(top, height + 8), pl.ds(base, 256))
            acc[spot] = acc[spot] + wide

    for j in range(count):
        planes = [jnp.concatenate([grad[0, j, c], grad[1, j, c]], axis=0) for c in range(2)]
        place(planes + [power], own_ref[0, 2 * j] - start + patch, own_ref[0, 2 * j + 1])
    for side, ref in ((0, from_above), (1, from_below)):
        for j in range(count):
            row = near_ref[side, 0, 2 * j] - start + patch + (half if side == 0 else 0)
            col = near_ref[side, 0, 2 * j + 1]

            @pl.when((row >= 0) & (row <= last - half))
            def _(side=side, ref=ref, j=j, row=row, col=col):
                part = power[half:] if side == 0 else power[:half]
                place([ref[j, 0], ref[j, 1], part], row, col)

    rows = pl.ds(patch, band)
    scale = acc[2, rows, :] + 1.0
    for c in range(2):
        out[0, c] = obj[0, c] + acc[c, rows, :] / scale


def final_kernel(n_ang, n_pos, new_obj, partial, weight, onehot,
                 recon, newp,
                 sino, tables, rh, rl, ag, piece,
                 local_sem, table_sem, a2a_send, a2a_recv, ag_send, ag_recv,
                 fin_send, fin_recv):
    me_a = lax.axis_index("angle")
    me_p = lax.axis_index("pos")
    ns = sino.shape[1]
    width = sino.shape[2]
    pr = piece.shape[1]
    chunk = tables.shape[2]
    per_row = width // chunk
    zwin = weight.shape[1]
    per_angle = zwin * per_row
    order = sorted(range(1, n_ang), key=lambda d: (min(d, n_ang - d), d))
    barrier = pltpu.get_barrier_semaphore()
    angle_peers = [lax.rem(me_a + d, n_ang) for d in order]
    pos_peers = [lax.rem(me_p + d, n_pos) for d in range(1, n_pos)]
    for peer in angle_peers:
        pl.semaphore_signal(barrier, inc=1, device_id={"angle": peer}, device_id_type=MESH)
    for peer in pos_peers:
        pl.semaphore_signal(barrier, inc=1, device_id={"pos": peer}, device_id_type=MESH)
    own = pltpu.make_async_copy(new_obj.at[0, 1, pl.ds(pl.multiple_of(me_a * ns, 8), ns), :],
                                sino.at[me_a], local_sem.at[0])
    own.start()
    sources = [me_a] + [lax.rem(me_a + n_ang - d, n_ang) for d in order]
    loads = []
    for k, a in enumerate(sources):
        span = pl.ds(a * per_angle, per_angle)
        loads.append(pltpu.make_async_copy(onehot.at[span], tables.at[span], table_sem.at[k]))
    loads[0].start()
    pl.semaphore_wait(barrier, n_ang + n_pos - 2)
    gather = [
        remote(partial, ag.at[me_a], ag_send.at[k], ag_recv.at[k], "angle", peer)
        for k, peer in enumerate(angle_peers)
    ]
    for copy in gather:
        copy.start()
    across = [
        remote(new_obj.at[0, 1, pl.ds(pl.multiple_of(peer * ns, 8), ns), :], sino.at[me_a],
               a2a_send.at[k], a2a_recv.at[k], "angle", peer)
        for k, peer in enumerate(angle_peers)
    ]
    for copy in across:
        copy.start()
    for copy in loads[1:]:
        copy.start()
    tall = 64

    def ramp(step, carry):
        top = pl.multiple_of(step * tall, tall)
        shape = (tall, width)
        differ = lax.broadcasted_iota(jnp.int32, shape, 1) - (
            lax.broadcasted_iota(jnp.int32, shape, 0) + top)
        spread = differ.astype(jnp.float32)
        odd = -1.0 / (jnp.maximum(spread * spread, 1.0) * (math.pi * math.pi))
        value = jnp.where((differ & 1) == 1, odd, jnp.where(differ == 0, 0.25, 0.0))
        rh[pl.ds(top, tall), :], rl[pl.ds(top, tall), :] = halves(value)
        return carry

    lax.fori_loop(0, width // tall, ramp, 0)

    def project(k):
        a = sources[k]
        high, low = halves(sino[a])
        both = mm(jnp.concatenate([high, low], axis=0), rh[...])
        lines = (both[:ns] + both[ns:] + mm(high, rl[...])) * (math.pi / n_ang)
        high, low = halves(lines)
        next_high, next_low = halves(pltpu.roll(lines, width - 1, 1))
        stack = jnp.concatenate([high, low, next_high, next_low], axis=0)
        loads[k].wait()
        for n in range(per_angle):
            z, part = n // per_row, n % per_row
            got = mm(stack, tables[a * per_angle + n])
            lower = got[:ns] + got[ns:2 * ns]
            upper = got[2 * ns:3 * ns] + got[3 * ns:]
            w = weight[pl.ds(a, 1), z, pl.ds(part * chunk, chunk)]
            value = (1.0 - w) * lower + w * upper
            lanes = pl.ds(n * chunk, chunk)
            recon[:, lanes] = value if k == 0 else recon[:, lanes] + value

    ag[me_a] = partial[...]
    for copy in gather:
        copy.wait()
    mine = pl.ds(pl.multiple_of(me_p * pr, 8), pr)
    whole = ag[0]
    for a in range(1, n_ang):
        whole = whole + ag[a]
    for c in range(2):
        value = whole[c] / (whole[2] + 1.0)
        piece[c] = value
        newp[c, mine, :] = value
    spread = [
        remote(piece, newp.at[:, mine, :], fin_send.at[d], fin_recv.at[d], "pos", peer)
        for d, peer in enumerate(pos_peers)
    ]
    for copy in spread:
        copy.start()
    own.wait()
    project(0)
    for k in range(1, n_ang):
        across[k - 1].wait()
        project(k)
    for copy in spread:
        copy.wait()


def on_device(n_ang, n_pos, amplitude, offsets, probe_field, object_field, interp_index, interp_weight):
    band = object_field.shape[2]
    width = object_field.shape[3]
    patch = probe_field.shape[1]
    half = patch // 2
    count = offsets.shape[1]
    f32, i32 = jnp.float32, jnp.int32
    start = lax.axis_index("pos").astype(i32) * band
    own = offsets[0]
    corner = own.T - jnp.where(jnp.arange(2)[:, None] == 0, start - half, 0)
    where_at = corner[::-1, :, None] + jnp.arange(patch, dtype=i32)[None, None, :]
    where_at = where_at.reshape(2, count * patch)
    padded = jnp.pad(own.reshape(1, 2 * count), ((0, 7), (0, 128 - 2 * count)))
    n_z = interp_index.shape[1]
    chunk = min(512, width)
    tables = n_ang * n_z * (width // chunk)
    bf16 = jnp.bfloat16
    left, right = dft_blocks(patch)
    ah, al = split_const(left)
    bh, bl = split_const(right)
    vmem = pl.BlockSpec(memory_space=VMEM)
    smem = pl.BlockSpec(memory_space=pltpu.SMEM)
    hbm = pl.BlockSpec(memory_space=pl.ANY)
    sds = jax.ShapeDtypeStruct
    dma = pltpu.SemaphoreType.DMA
    half_shape = (count, 2, half, patch)
    grad, from_above, from_below, near, partial, onehot = pl.pallas_call(
        functools.partial(patch_kernel, n_pos),
        out_shape=(
            sds((2,) + half_shape, f32), sds(half_shape, f32), sds(half_shape, f32),
            sds((2, 8, 128), i32), sds((3, patch // n_pos, patch), f32),
            sds((tables, width, chunk), bf16),
        ),
        in_specs=[vmem, hbm] + [vmem] * 8,
        out_specs=(vmem,) * 5 + (hbm,),
        scratch_shapes=[
            VMEM((2, band + patch, width), f32),
            VMEM((2, width, chunk), bf16),
            VMEM((3, patch, patch), f32),
            VMEM((n_pos - 1, 3, patch // n_pos, patch), f32),
            dma((1,)), dma((2,)), dma((4 + 2 * count,)), dma((4 + 2 * count,)), dma((n_pos - 1,)), dma((n_pos - 1,)),
        ],
        compiler_params=pltpu.CompilerParams(collective_id=0, has_side_effects=True),
        name="patches",
    )(where_at, object_field, padded, interp_index, amplitude[0], probe_field, ah, al, bh, bl)
    new_object = pl.pallas_call(
        functools.partial(merge_kernel, count),
        out_shape=sds(object_field.shape, f32),
        in_specs=[smem] * 3 + [vmem] * 5,
        out_specs=vmem,
        scratch_shapes=[VMEM((3, band + 2 * patch + 8, width), f32)],
        name="merge",
    )(start[None], padded, near, object_field, probe_field, grad, from_above, from_below)
    total = n_z * width
    ns = band // n_ang
    pr = patch // n_pos
    recon, change = pl.pallas_call(
        functools.partial(final_kernel, n_ang, n_pos),
        out_shape=(sds((ns, total), f32), sds(probe_field.shape, f32)),
        in_specs=[hbm] + [vmem] * 2 + [hbm],
        out_specs=(vmem, vmem),
        scratch_shapes=[
            VMEM((n_ang, ns, width), f32),
            VMEM((tables, width, chunk), bf16),
            VMEM((width, width), bf16), VMEM((width, width), bf16),
            VMEM((n_ang, 3, pr, patch), f32),
            VMEM((2, pr, patch), f32),
            dma((1,)), dma((n_ang,)),
            dma((n_ang - 1,)), dma((n_ang - 1,)),
            dma((n_ang - 1,)), dma((n_ang - 1,)),
            dma((n_pos - 1,)), dma((n_pos - 1,)),
        ],
        compiler_params=pltpu.CompilerParams(
            collective_id=1, has_side_effects=True, vmem_limit_bytes=BIG),
        name="final",
    )(new_object, partial, interp_weight, onehot)
    return new_object, probe_field + change, recon.reshape(1, ns, n_z, width)


def solution(mesh):
    placed = (
        P("angle", "pos", None, None),
        P("angle", "pos", None),
        P(),
        P("angle", None, "pos", None),
        P(),
        P(),
    )
    return jax.shard_map(
        functools.partial(on_device, mesh.shape["angle"], mesh.shape["pos"]),
        mesh=mesh,
        in_specs=placed,
        out_specs=(P("angle", None, "pos", None), P(), P("pos", "angle", None, None)),
        check_vma=False,
    )
```

profile of v0, /device:TPU:0, one launch (start us, length us, event | category | flops | bytes accessed | tf_op | source)
XLA Modules:
  0.0 64.7 jit_solution(13878417831856145351)
XLA Ops:
  0.6 0.0 copy-start
  0.7 0.8 %fusion = s32[2,4]{1,0:T(2,128)S(1)} fusion(s32[1,4,2]{1,2,0:T(2,128)} %param.11, s32[2]{0:T(128)S(1)} %compare_select_fusion), kind=kLoop, calls=%fused_computation.5 | loop fusion | flops 8 | bytes 72 | tf_op jit(solution)/shard_map/sub | solution.py:377
  1.5 0.8 %copy.14 = s32[1,4,2]{2,1,0:T(4,128)S(1)} copy(s32[1,4,2]{1,2,0:T(2,128)} %param.11) | data formatting | bytes 64 | tf_op args[1]
  2.2 0.1 reshape_squeeze.3
  2.3 0.1 broadcast_bitcast_fusion
  2.4 0.6 bitcast_add_fusion.where_at
  3.0 0.6 pad.4.offs.own_ref
  3.6 31.4 %patches.1 = (f32[2,4,2,64,128]{4,3,2,1,0:T(8,128)}, f32[4,2,64,128]{3,2,1,0:T(8,128)}, f32[4,2,64,128]{3,2,1,0:T(8,128)}, s32[2,8,128]{2,1,0:T(8,128)}, f32[3,1...) custom-call(s32[2,512]{1,0:T(2,128)} %bitcast_add_fusion.where_at, f32[1,2,128,1024]{3,2,1,0:T(8,128)} %obj.3, ...), custom_call_target="tpu_custom_call" | custom-call | tf_op jit(solution)/shard_map/patches/pallas_call | solution.py:394
  35.0 4.0 %merge.1.new_obj = f32[1,2,128,1024]{3,2,1,0:T(8,128)} custom-call(s32[1]{0:T(128)} %bitcast.start_ref, s32[8,128]{1,0:T(8,128)} %pad.4.offs.own_ref, s32[2,8,128]{2,1,0:T(8,128)} %get-tuple-element.11.near_ref, f32[1,2,128,1024]{3,2,1,0:T(8,128)} %obj.3, f32[2,128,128]{2,1,0:T(8,128)} %probe.3, f32[2,4,2,64,128]{4,3,2,1,0:T(8,128)} %get-tuple-element.12.grad, ...), custom_call_target="tpu_custom_call" | custom-call | tf_op jit(solution)/shard_map/merge/pallas_call | solution.py:413
  38.9 22.3 %final.1 = (f32[32,2048]{1,0:T(8,128)}, f32[2,128,128]{2,1,0:T(8,128)}) custom-call(f32[1,2,128,1024]{3,2,1,0:T(8,128)} %merge.1.new_obj, f32[3,16,128]{2,1,0:T(8,128)} %get-tuple-element.15.partial, f32[4,2,1024]{2,1,0:T(2,128)} %weight.1, bf16[16,1024,512]{2,1,0:T(8,128)(2,1)} %get-tuple-element.16.onehot), custom_call_target="tpu_custom_call" | custom-call | tf_op jit(solution)/shard_map/final/pallas_call | solution.py:424
  61.2 0.0 copy-done
  61.2 1.6 %add.32 = f32[2,128,128]{2,1,0:T(8,128)} add(f32[2,128,128]{2,1,0:T(8,128)S(1)} %copy-done, f32[2,128,128]{2,1,0:T(8,128)} %get-tuple-element.17) | non-fusion elementwise | flops 32768 | bytes 393216 | tf_op jit(solution)/shard_map/add | solution.py:444
  62.8 1.9 %reshape.20 = f32[1,32,2,1024]{3,2,1,0:T(2,128)} reshape(f32[32,2048]{1,0:T(8,128)} %get-tuple-element.18) | data formatting | bytes 524288 | tf_op jit(solution)/shard_map/reshape | solution.py:444
  (3 shorter events, 0.0 us)
Async XLA Ops:
  0.6 60.6 %copy-start = (f32[2,128,128]{2,1,0:T(8,128)S(1)}, f32[2,128,128]{2,1,0:T(8,128)}, u32[]{:S(2)}) copy-start(f32[2,128,128]{2,1,0:T(8,128)} %probe.3) | copy-start | bytes 393220
where the time goes:
time: 65 us; the launch traced here: 64.7 us
  Pallas kernels  57.6 us (89%)
  local copies, waits for them, and re-layouts  3.42 us (5%)
  other arithmetic  2.97 us (5%)
  between operations  0.68 us (1%)
    pallas_call x1, Pallas kernels, on_device(): pl.pallas_call(functools.partial(patch_kernel, n_pos), out_shape=(sds((2,...  31.4 us
    pallas_call x1, Pallas kernels, on_device(): pl.pallas_call(functools.partial(final_kernel, n_ang, n_pos), out_shape=(...  22.3 us
    pallas_call x1, Pallas kernels, on_device(): pl.pallas_call(functools.partial(merge_kernel, count), out_shape=sds(obje...  3.96 us
    reshape x1, local copies, waits for them, and re-layouts, on_device(): return (new_object, probe_field + change, recon.reshape(1, ns, n_z, width))  1.87 us
    add x1, other arithmetic, on_device(): return (new_object, probe_field + change, recon.reshape(1, ns, n_z, width))  1.57 us

commit v1 on v0

v1 whole, which is shorter than its diff:
```python
import functools
import math

import jax
import jax.numpy as jnp
import numpy as np
from jax import lax
from jax.experimental import pallas as pl
from jax.experimental.pallas import tpu as pltpu
from jax.sharding import PartitionSpec as P

MESH = pl.DeviceIdType.MESH
VMEM = pltpu.VMEM
LANES = 128


def split_const(table):
    high = jnp.asarray(table, jnp.float32).astype(jnp.bfloat16)
    low = (jnp.asarray(table, jnp.float32) - high.astype(jnp.float32)).astype(jnp.bfloat16)
    return high, low


def dft_blocks(length):
    ramp = np.arange(length)
    theta = (ramp[:, None] * ramp[None, :] % length) * (2.0 * math.pi / length)
    real = np.cos(theta) / math.sqrt(length)
    imag = -np.sin(theta) / math.sqrt(length)
    left = np.block([[real, -imag], [imag, real]])
    right = np.block([[real, imag], [-imag, real]])
    return np.asarray(left, np.float32), np.asarray(right, np.float32)


def halves(value):
    high = value.astype(jnp.bfloat16)
    return high, (value - high.astype(jnp.float32)).astype(jnp.bfloat16)


def mm(a, b):
    return jnp.dot(a, b, preferred_element_type=jnp.float32)


def left3(table_high, table_low, value):
    high, low = halves(value)
    return mm(table_high, high) + mm(table_high, low) + mm(table_low, high)


def right3(value, table_high, table_low):
    high, low = halves(value)
    return mm(high, table_high) + mm(low, table_high) + mm(high, table_low)


def remote(src, dst, send, recv, axis, target):
    return pltpu.make_async_remote_copy(
        src_ref=src, dst_ref=dst, send_sem=send, recv_sem=recv,
        device_id={axis: target}, device_id_type=MESH,
    )


def flip(me, mask, bits):
    other = 0
    for b in range(bits):
        bit = (me // (1 << b)) % 2
        other = other + (1 << b) * (1 - bit if (mask >> b) & 1 else bit)
    return other


def step_kernel(n_ang, n_pos, size,
                offs_h, obj_h, amp_h, probe_h, index_h, weight_h, ah_h, al_h, bh_h, bl_h,
                newobj, recon, change,
                offs, near, offs_v, near_v, obj, amp, probe, index, weight, ah, al, bh, bl,
                ext, sb, zo, za, zb, accw, acci, accr, grad, from_above, from_below,
                numden, rs, partial, ag, piece, sino, tables, rh, rl,
                in_sem, near_sem, send_sem, recv_sem, rs_send, rs_recv,
                a2a_send, a2a_recv, ag_send, ag_recv, fin_send, fin_recv):
    me_a = lax.axis_index("angle")
    me = lax.axis_index("pos")
    up, down = lax.rem(me + n_pos - 1, n_pos), lax.rem(me + 1, n_pos)
    tiles, band = obj.shape[1], obj.shape[2]
    width = tiles * LANES
    patch = probe.shape[1]
    half = patch // 2
    count = amp.shape[1]
    ns = sino.shape[1]

    sources = [(offs_h, offs), (offs_h, offs_v), (probe_h, probe), (amp_h, amp),
               (ah_h, ah), (al_h, al), (bh_h, bh), (bl_h, bl), (index_h, index), (weight_h, weight)]
    sources += [(obj_h.at[0, :, :, pl.ds(t * LANES, LANES)], obj.at[:, t]) for t in range(tiles)]
    loads = [pltpu.make_async_copy(src, dst, in_sem.at[k]) for k, (src, dst) in enumerate(sources)]
    for copy in loads:
        copy.start()
    bits = (n_ang - 1).bit_length()
    order = [1] + list(range(n_ang - 1, 1, -1))
    angle_peers = [flip(me_a, mask, bits) for mask in order]
    pos_peers = [lax.rem(me + d, n_pos) for d in range(1, n_pos)]
    barrier = pltpu.get_barrier_semaphore()
    for peer in pos_peers:
        pl.semaphore_signal(barrier, inc=1, device_id={"pos": peer}, device_id_type=MESH)
    for peer in angle_peers:
        pl.semaphore_signal(barrier, inc=1, device_id={"angle": peer}, device_id_type=MESH)
    loads[1].wait()
    pl.semaphore_wait(barrier, n_ang + n_pos - 2)
    swap = [remote(offs_v, near_v.at[0], send_sem.at[0], recv_sem.at[0], "pos", down),
            remote(offs_v, near_v.at[1], send_sem.at[1], recv_sem.at[1], "pos", up)]
    for copy in swap:
        copy.start()
    loads[0].wait()
    for copy in loads[10:]:
        copy.wait()

    def columns(c, rows, col):
        tile = col // LANES
        after = jnp.minimum(tile + 1, tiles - 1)
        got = jnp.concatenate([obj[c, tile, rows, :], obj[c, after, rows, :]], axis=1)
        return pltpu.roll(got, lax.rem(2 * LANES - lax.rem(col, LANES), 2 * LANES), 1)[:, :patch]

    for j in range(count):
        for c in range(2):
            ext[j // size][j % size, c, half:half + band, :] = columns(c, slice(0, band), offs[1, j])
    zo[...] = jnp.zeros_like(zo)
    za[...] = jnp.zeros_like(za)
    zb[...] = jnp.zeros_like(zb)
    for k, copy in enumerate(swap):
        copy.wait()
    for k in range(2):
        pltpu.make_async_copy(near_v.at[k], near.at[k], near_sem.at[k]).start()
    for k in range(2):
        pltpu.make_async_copy(near_v.at[k], near.at[k], near_sem.at[k]).wait()
    first = []
    groups = [range(g * size, (g + 1) * size) for g in range(count // size)]
    for g, group in enumerate(groups):
        for j in group:
            for c in range(2):
                sb[0, j, c] = columns(c, slice(band - half, band), near[1, 1, j])
                sb[1, j, c] = columns(c, slice(0, half), near[0, 1, j])
        span = pl.ds(g * size, size)
        pair = [
            remote(sb.at[0, span], ext[g].at[:, :, pl.ds(0, half), :],
                   send_sem.at[2 + 4 * g], recv_sem.at[2 + 4 * g], "pos", down),
            remote(sb.at[1, span], ext[g].at[:, :, pl.ds(half + band, half), :],
                   send_sem.at[3 + 4 * g], recv_sem.at[3 + 4 * g], "pos", up),
        ]
        for copy in pair:
            copy.start()
        first.append(pair)

    def spot(row, col, owner):
        return jnp.clip(row - owner * band + half, 0, band), col

    own_at = [spot(offs[0, j], offs[1, j], me) for j in range(count)]
    above_at = [spot(near[0, 0, j], near[0, 1, j], up) for j in range(count)]
    below_at = [spot(near[1, 0, j], near[1, 1, j], down) for j in range(count)]

    def wide(plane, col):
        blank = jnp.zeros((plane.shape[0], LANES), jnp.float32)
        both = jnp.concatenate([plane, blank], axis=1)
        return pltpu.roll(both, lax.rem(col, LANES), 1)

    lead = max(0, band - half)

    def place(acc, buf, first_row, plane, start, rows, col):
        shifted = wide(plane, col)
        where = slice(first_row, first_row + plane.shape[0])
        buf[tiles - 1, where, :] = shifted[:, :LANES]
        buf[tiles, where, :] = shifted[:, LANES:]
        begin = tiles - 1 - col // LANES
        for t in range(tiles):
            acc[t, rows, :] = acc[t, rows, :] + buf[begin + t, pl.ds(start, rows.stop - rows.start), :]

    def place_own(acc, plane, j):
        row, col = own_at[j]
        place(acc, zo, lead, plane, lead + half - row, slice(0, band), col)

    def place_above(acc, plane, j):
        row, col = above_at[j]
        place(acc, za, 0, plane, band - row, slice(0, half), col)

    def place_below(acc, plane, j):
        row, col = below_at[j]
        place(acc, zb, band, plane, band - row, slice(band - half, band), col)

    loads[2].wait()
    p_re, p_im = probe[0], probe[1]
    power = p_re * p_re + p_im * p_im
    accw[...] = jnp.ones_like(accw)
    acci[...] = jnp.zeros_like(acci)
    accr[...] = jnp.zeros_like(accr)
    for j in range(count):
        place_own(accw, power, j)
        place_above(accw, power[half:], j)
        place_below(accw, power[:half], j)
    accw[...] = 1.0 / accw[...]
    tall = 64

    def ramp(step, carry):
        top = pl.multiple_of(step * tall, tall)
        shape = (tall, width)
        differ = lax.broadcasted_iota(jnp.int32, shape, 1) - (
            lax.broadcasted_iota(jnp.int32, shape, 0) + top)
        spread = differ.astype(jnp.float32)
        odd = -1.0 / (jnp.maximum(spread * spread, 1.0) * (math.pi * math.pi))
        value = jnp.where((differ & 1) == 1, odd, jnp.where(differ == 0, 0.25, 0.0))
        rh[pl.ds(top, tall), :], rl[pl.ds(top, tall), :] = halves(value)
        return carry

    lax.fori_loop(0, width // tall, ramp, 0)
    for copy in loads[3:10]:
        copy.wait()
    n_re = jnp.zeros((patch, patch), jnp.float32)
    n_im = n_re
    den = n_re
    second = []
    for g, group in enumerate(groups):
        for copy in first[g]:
            copy.wait()
        q_re, q_im, w_re, w_im = [], [], [], []
        for j in group:
            rows = pl.ds(own_at[j][0], patch)
            re, im = ext[g][j % size, 0, rows, :], ext[g][j % size, 1, rows, :]
            q_re.append(re)
            q_im.append(im)
            w_re.append(p_re * re - p_im * im)
            w_im.append(p_re * im + p_im * re)
        psi = jnp.concatenate([jnp.concatenate(w_re, axis=1), jnp.concatenate(w_im, axis=1)], axis=0)
        mid = left3(ah[...], al[...], psi)
        cells = [slice(n * patch, (n + 1) * patch) for n in range(size)]
        rows = [jnp.concatenate([mid[:patch, cell], mid[patch:, cell]], axis=1) for cell in cells]
        spec = right3(jnp.concatenate(rows, axis=0), bh[...], bl[...])
        fixed = []
        for j, cell in zip(group, cells):
            s_re = spec[cell, :patch]
            s_im = spec[cell, patch:]
            factor = amp[0, j] / jnp.maximum(jnp.sqrt(s_re * s_re + s_im * s_im), 0.5)
            fixed.append(jnp.concatenate([factor * s_re, factor * s_im], axis=1))
        back = right3(jnp.concatenate(fixed, axis=0), ah[...], al[...])
        wide_re = jnp.concatenate([back[cell, :patch] for cell in cells], axis=1)
        wide_im = jnp.concatenate([back[cell, patch:] for cell in cells], axis=1)
        diff = left3(bh[...], bl[...], jnp.concatenate([wide_re, wide_im], axis=0))
        diff = diff - psi
        for n, j in enumerate(group):
            d_re, d_im = diff[:patch, cells[n]], diff[patch:, cells[n]]
            g_re = p_re * d_re + p_im * d_im
            g_im = p_re * d_im - p_im * d_re
            for h in range(2):
                grad[h, j, 0] = g_re[h * half:(h + 1) * half]
                grad[h, j, 1] = g_im[h * half:(h + 1) * half]
            n_re = n_re + (q_re[n] * d_re + q_im[n] * d_im)
            n_im = n_im + (q_re[n] * d_im - q_im[n] * d_re)
            den = den + (q_re[n] * q_re[n] + q_im[n] * q_im[n])
        span = pl.ds(g * size, size)
        pair = [
            remote(grad.at[1, span], from_above.at[span], send_sem.at[4 + 4 * g],
                   recv_sem.at[4 + 4 * g], "pos", down),
            remote(grad.at[0, span], from_below.at[span], send_sem.at[5 + 4 * g],
                   recv_sem.at[5 + 4 * g], "pos", up),
        ]
        for copy in pair:
            copy.start()
        second.append(pair)
    numden[0] = n_re
    numden[1] = n_im
    numden[2] = den
    pr = patch // n_pos
    scatter = [
        remote(numden.at[:, pl.ds(pl.multiple_of(peer * pr, 8), pr), :], rs.at[d],
               rs_send.at[d], rs_recv.at[d], "pos", peer)
        for d, peer in enumerate(pos_peers)
    ]
    for copy in scatter:
        copy.start()

    def whole_patch(j, c):
        return jnp.concatenate([grad[0, j, c], grad[1, j, c]], axis=0)

    for j in range(count):
        place_own(acci, whole_patch(j, 1), j)
    for g, group in enumerate(groups):
        for copy in second[g]:
            copy.wait()
        for j in group:
            place_above(acci, from_above[j, 1], j)
            place_below(acci, from_below[j, 1], j)
    for t in range(tiles):
        lanes = slice(t * LANES, (t + 1) * LANES)
        newobj[0, 1, :, lanes] = obj[1, t] + acci[t] * accw[t]
    across = [
        remote(newobj.at[0, 1, pl.ds(pl.multiple_of(peer * ns, 8), ns), :], sino.at[k],
               a2a_send.at[k], a2a_recv.at[k], "angle", peer)
        for k, peer in enumerate(angle_peers)
    ]
    for copy in across:
        copy.start()
    for j in range(count):
        place_own(accr, whole_patch(j, 0), j)
        place_above(accr, from_above[j, 0], j)
        place_below(accr, from_below[j, 0], j)
    for t in range(tiles):
        lanes = slice(t * LANES, (t + 1) * LANES)
        newobj[0, 0, :, lanes] = obj[0, t] + accr[t] * accw[t]
    for copy in scatter:
        copy.wait()
    part = numden[:, pl.ds(pl.multiple_of(me * pr, 8), pr), :]
    for d in range(n_pos - 1):
        part = part + rs[d]
    partial[...] = part
    gather = [
        remote(partial, ag.at[me_a], ag_send.at[k], ag_recv.at[k], "angle", peer)
        for k, peer in enumerate(angle_peers)
    ]
    for copy in gather:
        copy.start()

    chunk = tables.shape[2]
    per_row = width // chunk
    zwin = index.shape[1]
    per_angle = zwin * per_row
    bins = lax.broadcasted_iota(jnp.int32, (width, chunk), 0)

    def build(step, carry):
        a = step // per_angle
        z = lax.rem(step // per_row, zwin)
        lanes = pl.ds(pl.multiple_of(lax.rem(step, per_row) * chunk, chunk), chunk)
        hit = bins == index[a, pl.ds(z, 1), lanes]
        tables[step] = jnp.where(hit, 1.0, 0.0).astype(jnp.bfloat16)
        return carry

    lax.fori_loop(0, tables.shape[0], build, 0)

    def project(k, a, lines):
        high, low = halves(lines)
        both = mm(jnp.concatenate([high, low], axis=0), rh[...])
        lines = (both[:ns] + both[ns:] + mm(high, rl[...])) * (math.pi / n_ang)
        high, low = halves(lines)
        next_high, next_low = halves(pltpu.roll(lines, width - 1, 1))
        stack = jnp.concatenate([high, low, next_high, next_low], axis=0)
        for n in range(per_angle):
            z, part = n // per_row, n % per_row
            got = mm(stack, tables[a * per_angle + n])
            lower = got[:ns] + got[ns:2 * ns]
            upper = got[2 * ns:3 * ns] + got[3 * ns:]
            w = weight[pl.ds(a, 1), z, pl.ds(part * chunk, chunk)]
            value = (1.0 - w) * lower + w * upper
            lanes = pl.ds(n * chunk, chunk)
            recon[:, lanes] = value if k == 0 else recon[:, lanes] + value

    project(0, me_a, newobj[0, 1, pl.ds(pl.multiple_of(me_a * ns, 8), ns), :])
    ag[me_a] = partial[...]
    for copy in gather:
        copy.wait()
    total = ag[0]
    for a in range(1, n_ang):
        total = total + ag[a]
    mine = pl.ds(pl.multiple_of(me * pr, 8), pr)
    for c in range(2):
        value = total[c] / (total[2] + 1.0)
        piece[c] = value
        change[c, mine, :] = value
    spread = [
        remote(piece, change.at[:, mine, :], fin_send.at[d], fin_recv.at[d], "pos", peer)
        for d, peer in enumerate(pos_peers)
    ]
    for copy in spread:
        copy.start()
    for k, peer in enumerate(angle_peers):
        across[k].wait()
        project(k + 1, peer, sino[k])
    for copy in spread:
        copy.wait()


def tail_kernel(newobj, recon, change, probe, out_obj, out_probe, out_recon, sem):
    copy = pltpu.make_async_copy(newobj, out_obj, sem.at[0])
    copy.start()
    out_probe[...] = probe[...] + change[...]
    width = out_recon.shape[3]
    for s in range(out_recon.shape[1]):
        for z in range(out_recon.shape[2]):
            out_recon[0, s, z:z + 1, :] = recon[s:s + 1, z * width:(z + 1) * width]
    copy.wait()


def on_device(n_ang, n_pos, amplitude, offsets, probe_field, object_field, interp_index, interp_weight):
    band = object_field.shape[2]
    width = object_field.shape[3]
    patch = probe_field.shape[1]
    half = patch // 2
    count = offsets.shape[1]
    tiles = width // LANES
    f32, i32, bf16 = jnp.float32, jnp.int32, jnp.bfloat16
    n_z = interp_index.shape[1]
    chunk = min(512, width)
    tables = n_ang * n_z * (width // chunk)
    size = 2 if count % 2 == 0 else count
    left, right = dft_blocks(patch)
    ah, al = split_const(left)
    bh, bl = split_const(right)
    vmem = pl.BlockSpec(memory_space=VMEM)
    hbm = pl.BlockSpec(memory_space=pl.ANY)
    sds = jax.ShapeDtypeStruct
    dma = pltpu.SemaphoreType.DMA
    total = n_z * width
    ns = band // n_ang
    pr = patch // n_pos
    lead = max(0, band - half)
    ext = 2 * tiles
    table = VMEM((2 * patch, 2 * patch), bf16)
    half_shape = (count, 2, half, patch)
    links = 2 + 4 * (count // size)
    newobj, recon, change = pl.pallas_call(
        functools.partial(step_kernel, n_ang, n_pos, size),
        out_shape=(sds(object_field.shape, f32), sds((ns, total), f32), sds(probe_field.shape, f32)),
        in_specs=[hbm] * 10,
        out_specs=(vmem,) * 3,
        scratch_shapes=[
            pltpu.SMEM((2, count), i32), pltpu.SMEM((2, 2, count), i32),
            VMEM((2, count), i32), VMEM((2, 2, count), i32),
            VMEM((2, tiles, band, LANES), f32), VMEM(amplitude.shape, f32), VMEM(probe_field.shape, f32),
            VMEM(interp_index.shape, i32), VMEM(interp_weight.shape, f32),
            table, table, table, table,
            [VMEM((size, 2, band + patch, patch), f32)] * (count // size), VMEM((2,) + half_shape, f32),
            VMEM((ext, lead + half + band, LANES), f32),
            VMEM((ext, half + band, LANES), f32), VMEM((ext, half + band, LANES), f32),
            VMEM((tiles, band, LANES), f32), VMEM((tiles, band, LANES), f32), VMEM((tiles, band, LANES), f32),
            VMEM((2,) + half_shape, f32), VMEM(half_shape, f32), VMEM(half_shape, f32),
            VMEM((3, patch, patch), f32), VMEM((n_pos - 1, 3, pr, patch), f32),
            VMEM((3, pr, patch), f32), VMEM((n_ang, 3, pr, patch), f32), VMEM((2, pr, patch), f32),
            VMEM((n_ang - 1, ns, width), f32),
            VMEM((tables, width, chunk), bf16), VMEM((width, width), bf16), VMEM((width, width), bf16),
            dma((10 + tiles,)), dma((2,)), dma((links,)), dma((links,)), dma((n_pos - 1,)), dma((n_pos - 1,)),
            dma((n_ang - 1,)), dma((n_ang - 1,)), dma((n_ang - 1,)), dma((n_ang - 1,)),
            dma((n_pos - 1,)), dma((n_pos - 1,)),
        ],
        compiler_params=pltpu.CompilerParams(
            collective_id=0, has_side_effects=True, vmem_limit_bytes=KLIMIT),
        name="step",
    )(jnp.transpose(offsets[0]), object_field, amplitude, probe_field, interp_index, interp_weight, ah, al, bh, bl)
    out = pl.pallas_call(
        tail_kernel,
        out_shape=(sds(object_field.shape, f32), sds(probe_field.shape, f32), sds((1, ns, n_z, width), f32)),
        in_specs=[vmem] * 4,
        out_specs=(hbm, vmem, vmem),
        scratch_shapes=[dma((1,))],
        compiler_params=pltpu.CompilerParams(vmem_limit_bytes=TLIMIT),
        name="tail",
    )(newobj, recon, change, probe_field)
    return tuple(out)


KLIMIT = 56 * 1024 * 1024
TLIMIT = 8 * 1024 * 1024


def solution(mesh):
    placed = (
        P("angle", "pos", None, None),
        P("angle", "pos", None),
        P(),
        P("angle", None, "pos", None),
        P(),
        P(),
    )
    return jax.shard_map(
        functools.partial(on_device, mesh.shape["angle"], mesh.shape["pos"]),
        mesh=mesh,
        in_specs=placed,
        out_specs=(P("angle", None, "pos", None), P(), P("pos", "angle", None, None)),
        check_vma=False,
    )
```

time: 65 us -> 49.3 us (0.76)
  Pallas kernels: 57.6 us -> 45.3 us
  other arithmetic: 2.97 us -> 0 us
    pallas_call x3 -> x2, Pallas kernels: 57.6 us -> 45.3 us  [the longest x1 43.6 us: on_device(): pl.pallas_call(functools.partial(step_kernel, n_ang, n_pos, size), out_sh...]
    unnamed x4 -> x8, local copies, waits for them, and re-layouts: 0.84 us -> 3.08 us
    add x2 -> x0, other arithmetic: 2.18 us -> none  [the longest x1 1.57 us: on_device(): return (new_object, probe_field + change, recon.reshape(1, ns, n_z, width))]
    reshape x1 -> x0, local copies, waits for them, and re-layouts: 1.87 us -> none  [on_device(): return (new_object, probe_field + change, recon.reshape(1, ns, n_z, width))]
    sub x1 -> x0, other arithmetic: 0.78 us -> none  [on_device(): corner = own.T - jnp.where(jnp.arange(2)[:, None] == 0, start - half, 0)]
where the time goes in v1:
time: 49.3 us; the launch traced here: 49.1 us
  Pallas kernels  45.3 us (92%)
  local copies, waits for them, and re-layouts  3.08 us (6%)
  between operations  0.67 us (1%)
    pallas_call x1, Pallas kernels, on_device(): pl.pallas_call(functools.partial(step_kernel, n_ang, n_pos, size), out_sh...  43.6 us
    unnamed x8, local copies, waits for them, and re-layouts  3.08 us
    pallas_call x1, Pallas kernels, on_device(): pl.pallas_call(tail_kernel, out_shape=(sds(object_field.shape, f32), sds(...  1.72 us

profile of v1, /device:TPU:0, one launch (start us, length us, event | category | flops | bytes accessed | tf_op | source)
XLA Modules:
  0.0 49.1 jit_solution(8223460535376123557)
XLA Ops:
  0.6 0.0 copy-start.1
  0.6 43.6 %step.1 = (f32[1,2,128,1024]{3,2,1,0:T(8,128)}, f32[32,2048]{1,0:T(8,128)}, f32[2,128,128]{2,1,0:T(8,128)}) custom-call(s32[2,4]{1,0:T(2,128)} %bitcast.3, f32[1,2,128,1024]{3,2,1,0:T(8,128)} %obj_h.1, f32[1,4,128,128]{3,2,1,0:T(8,128)} %amp_h.1, f32[2,128,128]{2,1,0:T(8,128)} %probe.1, s32[4,2,1024]{2,1,0:T(2,128)} %index_h.1, f32[4,2,1024]{2,1,0:T(2,128)} %weight_h.1, ...), custom_call_target="tpu_custom_call" | custom-call | tf_op jit(solution)/shard_map/step/pallas_call | solution.py:408
  44.3 0.0 copy-done.1
  44.3 0.0 copy-start
  44.3 1.2 %copy-done = f32[1,2,128,1024]{3,2,1,0:T(8,128)S(1)} copy-done((f32[1,2,128,1024]{3,2,1,0:T(8,128)S(1)}, f32[1,2,128,1024]{3,2,1,0:T(8,128)}, u32[]{:S(2)}) %copy-start) | copy-done | bytes 1048600
  45.5 0.0 copy-start.2
  45.5 0.9 %copy-done.2 = f32[32,2048]{1,0:T(8,128)S(1)} copy-done((f32[32,2048]{1,0:T(8,128)S(1)}, f32[32,2048]{1,0:T(8,128)}, u32[]{:S(2)}) %copy-start.2) | copy-done | bytes 262168
  46.4 0.0 copy-start.3
  46.4 0.9 %copy-done.3 = f32[2,128,128]{2,1,0:T(8,128)S(1)} copy-done((f32[2,128,128]{2,1,0:T(8,128)S(1)}, f32[2,128,128]{2,1,0:T(8,128)}, u32[]{:S(2)}) %copy-start.3) | copy-done | bytes 131096
  47.3 1.7 %tail.1 = (f32[1,2,128,1024]{3,2,1,0:T(8,128)}, f32[2,128,128]{2,1,0:T(8,128)}, f32[1,32,2,1024]{3,2,1,0:T(2,128)}) custom-call(f32[1,2,128,1024]{3,2,1,0:T(8,128)S(1)} %copy-done, f32[32,2048]{1,0:T(8,128)S(1)} %copy-done.2, f32[2,128,128]{2,1,0:T(8,128)S(1)} %copy-done.3, f32[2,128,128]{2,1,0:T(8,128)S(1)} %copy-done.1), custom_call_target="tpu_custom_call" | custom-call | tf_op jit(solution)/shard_map/tail/pallas_call | solution.py:436
Async XLA Ops:
  0.6 43.6 %copy-start.1 = (f32[2,128,128]{2,1,0:T(8,128)S(1)}, f32[2,128,128]{2,1,0:T(8,128)}, u32[]{:S(2)}) copy-start(f32[2,128,128]{2,1,0:T(8,128)} %probe.1) | copy-start | bytes 393220
  44.3 1.2 %copy-start = (f32[1,2,128,1024]{3,2,1,0:T(8,128)S(1)}, f32[1,2,128,1024]{3,2,1,0:T(8,128)}, u32[]{:S(2)}) copy-start(f32[1,2,128,1024]{3,2,1,0:T(8,128)} %get-tuple-element.6.newobj) | copy-start | bytes 3145732
  45.5 0.9 %copy-start.2 = (f32[32,2048]{1,0:T(8,128)S(1)}, f32[32,2048]{1,0:T(8,128)}, u32[]{:S(2)}) copy-start(f32[32,2048]{1,0:T(8,128)} %get-tuple-element.7.recon) | copy-start | bytes 786436
  46.4 0.9 %copy-start.3 = (f32[2,128,128]{2,1,0:T(8,128)S(1)}, f32[2,128,128]{2,1,0:T(8,128)}, u32[]{:S(2)}) copy-start(f32[2,128,128]{2,1,0:T(8,128)} %get-tuple-element.8.change) | copy-start | bytes 393220

commit v2 on v1

--- a/solution.py
+++ b/solution.py
@@ -67,10 +67,10 @@
 def step_kernel(n_ang, n_pos, size,
                 offs_h, obj_h, amp_h, probe_h, index_h, weight_h, ah_h, al_h, bh_h, bl_h,
                 newobj, recon, change,
-                offs, near, offs_v, near_v, obj, amp, probe, index, weight, ah, al, bh, bl,
+                offs, near, obj, amp, probe, index, weight, ah, al, bh, bl,
                 ext, sb, zo, za, zb, accw, acci, accr, grad, from_above, from_below,
                 numden, rs, partial, ag, piece, sino, tables, rh, rl,
-                in_sem, near_sem, send_sem, recv_sem, rs_send, rs_recv,
+                in_sem, send_sem, recv_sem, rs_send, rs_recv,
                 a2a_send, a2a_recv, ag_send, ag_recv, fin_send, fin_recv):
     me_a = lax.axis_index("angle")
     me = lax.axis_index("pos")
@@ -82,7 +82,7 @@
     count = amp.shape[1]
     ns = sino.shape[1]
 
-    sources = [(offs_h, offs), (offs_h, offs_v), (probe_h, probe), (amp_h, amp),
+    sources = [(offs_h, offs), (probe_h, probe), (amp_h, amp),
                (ah_h, ah), (al_h, al), (bh_h, bh), (bl_h, bl), (index_h, index), (weight_h, weight)]
     sources += [(obj_h.at[0, :, :, pl.ds(t * LANES, LANES)], obj.at[:, t]) for t in range(tiles)]
     loads = [pltpu.make_async_copy(src, dst, in_sem.at[k]) for k, (src, dst) in enumerate(sources)]
@@ -97,14 +97,13 @@
         pl.semaphore_signal(barrier, inc=1, device_id={"pos": peer}, device_id_type=MESH)
     for peer in angle_peers:
         pl.semaphore_signal(barrier, inc=1, device_id={"angle": peer}, device_id_type=MESH)
-    loads[1].wait()
+    loads[0].wait()
     pl.semaphore_wait(barrier, n_ang + n_pos - 2)
-    swap = [remote(offs_v, near_v.at[0], send_sem.at[0], recv_sem.at[0], "pos", down),
-            remote(offs_v, near_v.at[1], send_sem.at[1], recv_sem.at[1], "pos", up)]
+    swap = [remote(offs, near.at[0], send_sem.at[0], recv_sem.at[0], "pos", down),
+            remote(offs, near.at[1], send_sem.at[1], recv_sem.at[1], "pos", up)]
     for copy in swap:
         copy.start()
-    loads[0].wait()
-    for copy in loads[10:]:
+    for copy in loads[9:]:
         copy.wait()
 
     def columns(c, rows, col):
@@ -121,10 +120,6 @@
     zb[...] = jnp.zeros_like(zb)
     for k, copy in enumerate(swap):
         copy.wait()
-    for k in range(2):
-        pltpu.make_async_copy(near_v.at[k], near.at[k], near_sem.at[k]).start()
-    for k in range(2):
-        pltpu.make_async_copy(near_v.at[k], near.at[k], near_sem.at[k]).wait()
     first = []
     groups = [range(g * size, (g + 1) * size) for g in range(count // size)]
     for g, group in enumerate(groups):
@@ -135,9 +130,9 @@
         span = pl.ds(g * size, size)
         pair = [
             remote(sb.at[0, span], ext[g].at[:, :, pl.ds(0, half), :],
-                   send_sem.at[2 + 4 * g], recv_sem.at[2 + 4 * g], "pos", down),
+                   send_sem.at[2 + 6 * g], recv_sem.at[2 + 6 * g], "pos", down),
             remote(sb.at[1, span], ext[g].at[:, :, pl.ds(half + band, half), :],
-                   send_sem.at[3 + 4 * g], recv_sem.at[3 + 4 * g], "pos", up),
+                   send_sem.at[3 + 6 * g], recv_sem.at[3 + 6 * g], "pos", up),
         ]
         for copy in pair:
             copy.start()
@@ -178,7 +173,7 @@
         row, col = below_at[j]
         place(acc, zb, band, plane, band - row, slice(band - half, band), col)
 
-    loads[2].wait()
+    loads[1].wait()
     p_re, p_im = probe[0], probe[1]
     power = p_re * p_re + p_im * p_im
     accw[...] = jnp.ones_like(accw)
@@ -203,8 +198,34 @@
         return carry
 
     lax.fori_loop(0, width // tall, ramp, 0)
-    for copy in loads[3:10]:
+    for copy in loads[2:9]:
         copy.wait()
+    chunk = tables.shape[2]
+    per_row = width // chunk
+    zwin = index.shape[1]
+    per_angle = zwin * per_row
+    deep = 16
+    pattern = lax.broadcasted_iota(jnp.int32, (deep, chunk), 0)
+    one, zero = jnp.ones((deep, chunk), jnp.bfloat16), jnp.zeros((deep, chunk), jnp.bfloat16)
+    pattern = pattern.astype(jnp.int16)
+
+    origins = [me_a] + angle_peers
+
+    def build(k, step, carry):
+        a = origins[k]
+        z = step // per_row
+        lanes = pl.ds(pl.multiple_of(lax.rem(step, per_row) * chunk, chunk), chunk)
+        at = jnp.broadcast_to(index[a, pl.ds(z, 1), lanes], (deep, chunk)).astype(jnp.int16)
+        for r in range(width // deep):
+            hit = at == pattern + jnp.int16(r * deep)
+            tables[k * per_angle + step, r * deep:(r + 1) * deep, :] = jnp.where(hit, one, zero)
+        return carry
+
+    def build_all(k):
+        lax.fori_loop(0, per_angle, functools.partial(build, k), 0)
+
+    for k in range(n_ang):
+        build_all(k)
     n_re = jnp.zeros((patch, patch), jnp.float32)
     n_im = n_re
     den = n_re
@@ -247,15 +268,16 @@
             n_im = n_im + (q_re[n] * d_im - q_im[n] * d_re)
             den = den + (q_re[n] * q_re[n] + q_im[n] * q_im[n])
         span = pl.ds(g * size, size)
-        pair = [
-            remote(grad.at[1, span], from_above.at[span], send_sem.at[4 + 4 * g],
-                   recv_sem.at[4 + 4 * g], "pos", down),
-            remote(grad.at[0, span], from_below.at[span], send_sem.at[5 + 4 * g],
-                   recv_sem.at[5 + 4 * g], "pos", up),
-        ]
-        for copy in pair:
+        pairs = []
+        for c in (1, 0):
+            k = 4 + 6 * g + 2 * (1 - c)
+            pairs.append([
+                remote(grad.at[1, span, c], from_above.at[span, c], send_sem.at[k], recv_sem.at[k], "pos", down),
+                remote(grad.at[0, span, c], from_below.at[span, c], send_sem.at[k + 1], recv_sem.at[k + 1], "pos", up),
+            ])
+        for copy in pairs[0] + ([] if g == len(groups) - 1 else pairs[1]):
             copy.start()
-        second.append(pair)
+        second.append(pairs)
     numden[0] = n_re
     numden[1] = n_im
     numden[2] = den
@@ -265,7 +287,7 @@
                rs_send.at[d], rs_recv.at[d], "pos", peer)
         for d, peer in enumerate(pos_peers)
     ]
-    for copy in scatter:
+    for copy in scatter + second[-1][1]:
         copy.start()
 
     def whole_patch(j, c):
@@ -274,7 +296,7 @@
     for j in range(count):
         place_own(acci, whole_patch(j, 1), j)
     for g, group in enumerate(groups):
-        for copy in second[g]:
+        for copy in second[g][0]:
             copy.wait()
         for j in group:
             place_above(acci, from_above[j, 1], j)
@@ -282,49 +304,6 @@
     for t in range(tiles):
         lanes = slice(t * LANES, (t + 1) * LANES)
         newobj[0, 1, :, lanes] = obj[1, t] + acci[t] * accw[t]
-    across = [
-        remote(newobj.at[0, 1, pl.ds(pl.multiple_of(peer * ns, 8), ns), :], sino.at[k],
-               a2a_send.at[k], a2a_recv.at[k], "angle", peer)
-        for k, peer in enumerate(angle_peers)
-    ]
-    for copy in across:
-        copy.start()
-    for j in range(count):
-        place_own(accr, whole_patch(j, 0), j)
-        place_above(accr, from_above[j, 0], j)
-        place_below(accr, from_below[j, 0], j)
-    for t in range(tiles):
-        lanes = slice(t * LANES, (t + 1) * LANES)
-        newobj[0, 0, :, lanes] = obj[0, t] + accr[t] * accw[t]
-    for copy in scatter:
-        copy.wait()
-    part = numden[:, pl.ds(pl.multiple_of(me * pr, 8), pr), :]
-    for d in range(n_pos - 1):
-        part = part + rs[d]
-    partial[...] = part
-    gather = [
-        remote(partial, ag.at[me_a], ag_send.at[k], ag_recv.at[k], "angle", peer)
-        for k, peer in enumerate(angle_peers)
-    ]
-    for copy in gather:
-        copy.start()
-
-    chunk = tables.shape[2]
-    per_row = width // chunk
-    zwin = index.shape[1]
-    per_angle = zwin * per_row
-    bins = lax.broadcasted_iota(jnp.int32, (width, chunk), 0)
-
-    def build(step, carry):
-        a = step // per_angle
-        z = lax.rem(step // per_row, zwin)
-        lanes = pl.ds(pl.multiple_of(lax.rem(step, per_row) * chunk, chunk), chunk)
-        hit = bins == index[a, pl.ds(z, 1), lanes]
-        tables[step] = jnp.where(hit, 1.0, 0.0).astype(jnp.bfloat16)
-        return carry
-
-    lax.fori_loop(0, tables.shape[0], build, 0)
-
     def project(k, a, lines):
         high, low = halves(lines)
         both = mm(jnp.concatenate([high, low], axis=0), rh[...])
@@ -334,7 +313,7 @@
         stack = jnp.concatenate([high, low, next_high, next_low], axis=0)
         for n in range(per_angle):
             z, part = n // per_row, n % per_row
-            got = mm(stack, tables[a * per_angle + n])
+            got = mm(stack, tables[k * per_angle + n])
             lower = got[:ns] + got[ns:2 * ns]
             upper = got[2 * ns:3 * ns] + got[3 * ns:]
             w = weight[pl.ds(a, 1), z, pl.ds(part * chunk, chunk)]
@@ -342,13 +321,54 @@
             lanes = pl.ds(n * chunk, chunk)
             recon[:, lanes] = value if k == 0 else recon[:, lanes] + value
 
+    across = [
+        remote(newobj.at[0, 1, pl.ds(pl.multiple_of(peer * ns, 8), ns), :], sino.at[k],
+               a2a_send.at[k], a2a_recv.at[k], "angle", peer)
+        for k, peer in enumerate(angle_peers)
+    ]
+    inner = (me_a >= n_ang // 4) & (me_a < n_ang - n_ang // 4)
+    across[0].start()
+
+    @pl.when(inner)
+    def _():
+        for copy in across[1:-1]:
+            copy.start()
+
+    for copy in scatter:
+        copy.wait()
+    part = numden[:, pl.ds(pl.multiple_of(me * pr, 8), pr), :]
+    for d in range(n_pos - 1):
+        part = part + rs[d]
+    partial[0] = part
+    shares = [
+        remote(partial.at[b], ag.at[b], ag_send.at[b], ag_recv.at[b], "angle", flip(me_a, 1 << b, bits))
+        for b in range(bits)
+    ]
+    shares[0].start()
+
+    @pl.when(jnp.logical_not(inner))
+    def _():
+        for copy in across[1:-1]:
+            copy.start()
+
     project(0, me_a, newobj[0, 1, pl.ds(pl.multiple_of(me_a * ns, 8), ns), :])
-    ag[me_a] = partial[...]
-    for copy in gather:
-        copy.wait()
-    total = ag[0]
-    for a in range(1, n_ang):
-        total = total + ag[a]
+    for b in range(bits - 1):
+        shares[b].wait()
+        partial[b + 1] = partial[b] + ag[b]
+        shares[b + 1].start()
+    across[-1].start()
+    for g, group in enumerate(groups):
+        for copy in second[g][1]:
+            copy.wait()
+        for j in group:
+            place_own(accr, whole_patch(j, 0), j)
+            place_above(accr, from_above[j, 0], j)
+            place_below(accr, from_below[j, 0], j)
+    for t in range(tiles):
+        lanes = slice(t * LANES, (t + 1) * LANES)
+        newobj[0, 0, :, lanes] = obj[0, t] + accr[t] * accw[t]
+    shares[-1].wait()
+    total = partial[bits - 1] + ag[bits - 1]
     mine = pl.ds(pl.multiple_of(me * pr, 8), pr)
     for c in range(2):
         value = total[c] / (total[2] + 1.0)
@@ -404,15 +424,15 @@
     ext = 2 * tiles
     table = VMEM((2 * patch, 2 * patch), bf16)
     half_shape = (count, 2, half, patch)
-    links = 2 + 4 * (count // size)
+    bits = (n_ang - 1).bit_length()
+    links = 2 + 6 * (count // size)
     newobj, recon, change = pl.pallas_call(
         functools.partial(step_kernel, n_ang, n_pos, size),
-        out_shape=(sds(object_field.shape, f32), sds((ns, total), f32), sds(probe_field.shape, f32)),
+        out_shape=(VMEM(object_field.shape, f32), VMEM((ns, total), f32), VMEM(probe_field.shape, f32)),
         in_specs=[hbm] * 10,
         out_specs=(vmem,) * 3,
         scratch_shapes=[
             pltpu.SMEM((2, count), i32), pltpu.SMEM((2, 2, count), i32),
-            VMEM((2, count), i32), VMEM((2, 2, count), i32),
             VMEM((2, tiles, band, LANES), f32), VMEM(amplitude.shape, f32), VMEM(probe_field.shape, f32),
             VMEM(interp_index.shape, i32), VMEM(interp_weight.shape, f32),
             table, table, table, table,
@@ -422,17 +442,19 @@
             VMEM((tiles, band, LANES), f32), VMEM((tiles, band, LANES), f32), VMEM((tiles, band, LANES), f32),
             VMEM((2,) + half_shape, f32), VMEM(half_shape, f32), VMEM(half_shape, f32),
             VMEM((3, patch, patch), f32), VMEM((n_pos - 1, 3, pr, patch), f32),
-            VMEM((3, pr, patch), f32), VMEM((n_ang, 3, pr, patch), f32), VMEM((2, pr, patch), f32),
+            VMEM((bits, 3, pr, patch), f32), VMEM((bits, 3, pr, patch), f32), VMEM((2, pr, patch), f32),
             VMEM((n_ang - 1, ns, width), f32),
             VMEM((tables, width, chunk), bf16), VMEM((width, width), bf16), VMEM((width, width), bf16),
-            dma((10 + tiles,)), dma((2,)), dma((links,)), dma((links,)), dma((n_pos - 1,)), dma((n_pos - 1,)),
-            dma((n_ang - 1,)), dma((n_ang - 1,)), dma((n_ang - 1,)), dma((n_ang - 1,)),
+            dma((9 + tiles,)), dma((links,)), dma((links,)), dma((n_pos - 1,)), dma((n_pos - 1,)),
+            dma((n_ang - 1,)), dma((n_ang - 1,)), dma((bits,)), dma((bits,)),
             dma((n_pos - 1,)), dma((n_pos - 1,)),
         ],
         compiler_params=pltpu.CompilerParams(
             collective_id=0, has_side_effects=True, vmem_limit_bytes=KLIMIT),
         name="step",
-    )(jnp.transpose(offsets[0]), object_field, amplitude, probe_field, interp_index, interp_weight, ah, al, bh, bl)
+    )(*(pltpu.with_memory_space_constraint(x, pltpu.HBM) for x in (
+        jnp.transpose(offsets[0]), object_field, amplitude, probe_field, interp_index, interp_weight,
+        ah, al, bh, bl)))
     out = pl.pallas_call(
         tail_kernel,
         out_shape=(sds(object_field.shape, f32), sds(probe_field.shape, f32), sds((1, ns, n_z, width), f32)),
@@ -445,7 +467,7 @@
     return tuple(out)
 
 
-KLIMIT = 56 * 1024 * 1024
+KLIMIT = 48 * 1024 * 1024
 TLIMIT = 8 * 1024 * 1024
 
 

time: 49.3 us -> 42.3 us (0.86)
  Pallas kernels: 45.3 us -> 41.5 us
  local copies, waits for them, and re-layouts: 3.08 us -> 0.01 us
    pallas_call x1, Pallas kernels: 43.6 us -> 39.8 us  [on_device(): pl.pallas_call(functools.partial(step_kernel, n_ang, n_pos, size), out_sh...]
    unnamed x8 -> x2, local copies, waits for them, and re-layouts: 3.08 us -> 0.01 us
where the time goes in v2:
time: 42.3 us; the launch traced here: 42.1 us
  Pallas kernels  41.5 us (98%)
  between operations  0.66 us (2%)
    pallas_call x1, Pallas kernels, on_device(): pl.pallas_call(functools.partial(step_kernel, n_ang, n_pos, size), out_sh...  39.8 us
    pallas_call x1, Pallas kernels, on_device(): pl.pallas_call(tail_kernel, out_shape=(sds(object_field.shape, f32), sds(...  1.73 us

profile of v2, /device:TPU:0, one launch (start us, length us, event | category | flops | bytes accessed | tf_op | source)
XLA Modules:
  0.0 42.1 jit_solution(13534164101692704609)
XLA Ops:
  0.6 0.0 copy-start
  0.6 39.8 %step.1 = (f32[1,2,128,1024]{3,2,1,0:T(8,128)S(1)}, f32[32,2048]{1,0:T(8,128)S(1)}, f32[2,128,128]{2,1,0:T(8,128)S(1)}) custom-call(s32[2,4]{1,0:T(2,128)} %bitcast.3, f32[1,2,128,1024]{3,2,1,0:T(8,128)} %obj_h.1, f32[1,4,128,128]{3,2,1,0:T(8,128)} %amp_h.1, f32[2,128,128]{2,1,0:T(8,128)} %probe.1, s32[4,2,1024]{2,1,0:T(2,128)} %index_h.1, ...), custom_call_target="tpu_custom_call" | custom-call | tf_op jit(solution)/shard_map/step/pallas_call | solution.py:429
  40.4 0.0 copy-done
  40.4 1.7 %tail.1 = (f32[1,2,128,1024]{3,2,1,0:T(8,128)}, f32[2,128,128]{2,1,0:T(8,128)}, f32[1,32,2,1024]{3,2,1,0:T(2,128)}) custom-call(f32[1,2,128,1024]{3,2,1,0:T(8,128)S(1)} %get-tuple-element.6.newobj, f32[32,2048]{1,0:T(8,128)S(1)} %get-tuple-element.7.recon, f32[2,128,128]{2,1,0:T(8,128)S(1)} %get-tuple-element.8.change, f32[2,128,128]{2,1,0:T(8,128)S(1)} %copy-done), custom_call_target="tpu_custom_call" | custom-call | tf_op jit(solution)/shard_map/tail/pallas_call | solution.py:458
Async XLA Ops:
  0.6 39.8 %copy-start = (f32[2,128,128]{2,1,0:T(8,128)S(1)}, f32[2,128,128]{2,1,0:T(8,128)}, u32[]{:S(2)}) copy-start(f32[2,128,128]{2,1,0:T(8,128)} %probe.1) | copy-start | bytes 393220

commit v3 on v2

--- a/solution.py
+++ b/solution.py
@@ -387,6 +387,409 @@
         copy.wait()
 
 
+def slice_kernel(n_ang, n_pos, size,
+                 offs_h, obj_h, amp_h, probe_h, index_h, weight_h, ah_h, al_h, bh_h, bl_h,
+                 newobj, recon, change,
+                 offs, near, far, farn, obj, amp, probe, index, weight, ah, al, bh, bl,
+                 ext, sb, zo, za, zb, zq, accw, acci, accr, grad, from_above, from_below,
+                 twice, blk, orx, rx, nrx, lw, lg,
+                 numden, rs, partial, ag, piece, tables, rh, rl,
+                 in_sem, send_sem, recv_sem, rs_send, rs_recv, far_send, far_recv, farn_send, farn_recv,
+                 o_send, o_recv, z_send, z_recv, f_send, f_recv, ag_send, ag_recv, fin_send, fin_recv):
+    me_a = lax.axis_index("angle")
+    me = lax.axis_index("pos")
+    up, down = lax.rem(me + n_pos - 1, n_pos), lax.rem(me + 1, n_pos)
+    tiles, band = obj.shape[1], obj.shape[2]
+    width = tiles * LANES
+    patch = probe.shape[1]
+    half = patch // 2
+    count = amp.shape[1]
+    ns = orx.shape[2]
+    side = (me_a * ns) // half
+    ahead = lax.rem(me + n_pos + 1 - 2 * side, n_pos)
+    behind = lax.rem(me + n_pos - 1 + 2 * side, n_pos)
+
+    sources = [(offs_h, offs), (probe_h, probe), (amp_h, amp),
+               (ah_h, ah), (al_h, al), (bh_h, bh), (bl_h, bl), (index_h, index), (weight_h, weight)]
+    sources += [(obj_h.at[0, :, :, pl.ds(t * LANES, LANES)], obj.at[:, t]) for t in range(tiles)]
+    loads = [pltpu.make_async_copy(src, dst, in_sem.at[k]) for k, (src, dst) in enumerate(sources)]
+    for copy in loads:
+        copy.start()
+    bits = (n_ang - 1).bit_length()
+    order = [1] + list(range(n_ang - 1, 1, -1))
+    angle_peers = [flip(me_a, mask, bits) for mask in order]
+    pos_peers = [lax.rem(me + d, n_pos) for d in range(1, n_pos)]
+    barrier = pltpu.get_barrier_semaphore()
+    for peer in pos_peers:
+        pl.semaphore_signal(barrier, inc=1, device_id={"pos": peer}, device_id_type=MESH)
+    for peer in angle_peers:
+        pl.semaphore_signal(barrier, inc=1, device_id={"angle": peer}, device_id_type=MESH)
+    loads[0].wait()
+    pl.semaphore_wait(barrier, n_ang + n_pos - 2)
+    swap = [remote(offs, near.at[0], send_sem.at[0], recv_sem.at[0], "pos", down),
+            remote(offs, near.at[1], send_sem.at[1], recv_sem.at[1], "pos", up)]
+    reach = [remote(offs, far.at[n], far_send.at[n], far_recv.at[n], "angle", peer)
+             for n, peer in enumerate(angle_peers)]
+    for copy in swap + reach:
+        copy.start()
+    for copy in loads[9:]:
+        copy.wait()
+    early = [remote(obj.at[1, :, pl.ds(pl.multiple_of(peer * ns, 8), ns), :], orx.at[n],
+                    o_send.at[n], o_recv.at[n], "angle", peer)
+             for n, peer in enumerate(angle_peers)]
+    for copy in early:
+        copy.start()
+
+    def columns(c, rows, col):
+        tile = col // LANES
+        after = jnp.minimum(tile + 1, tiles - 1)
+        got = jnp.concatenate([obj[c, tile, rows, :], obj[c, after, rows, :]], axis=1)
+        return pltpu.roll(got, lax.rem(2 * LANES - lax.rem(col, LANES), 2 * LANES), 1)[:, :patch]
+
+    for j in range(count):
+        for c in range(2):
+            ext[j // size][j % size, c, half:half + band, :] = columns(c, slice(0, band), offs[1, j])
+    zo[...] = jnp.zeros_like(zo)
+    za[...] = jnp.zeros_like(za)
+    zb[...] = jnp.zeros_like(zb)
+    zq[...] = jnp.zeros_like(zq)
+    lg[...] = jnp.zeros_like(lg)
+    lw[...] = jnp.ones_like(lw)
+    for k, copy in enumerate(swap):
+        copy.wait()
+    first = []
+    groups = [range(g * size, (g + 1) * size) for g in range(count // size)]
+    for g, group in enumerate(groups):
+        for j in group:
+            for c in range(2):
+                sb[0, j, c] = columns(c, slice(band - half, band), near[1, 1, j])
+                sb[1, j, c] = columns(c, slice(0, half), near[0, 1, j])
+        span = pl.ds(g * size, size)
+        pair = [
+            remote(sb.at[0, span], ext[g].at[:, :, pl.ds(0, half), :],
+                   send_sem.at[2 + 6 * g], recv_sem.at[2 + 6 * g], "pos", down),
+            remote(sb.at[1, span], ext[g].at[:, :, pl.ds(half + band, half), :],
+                   send_sem.at[3 + 6 * g], recv_sem.at[3 + 6 * g], "pos", up),
+        ]
+        for copy in pair:
+            copy.start()
+        first.append(pair)
+    relay = [remote(far.at[n], farn.at[n], farn_send.at[n], farn_recv.at[n], "pos", ahead)
+             for n in range(n_ang - 1)]
+    for n in range(n_ang - 1):
+        reach[n].wait()
+        relay[n].start()
+
+    def spot(row, col, owner):
+        return jnp.clip(row - owner * band + half, 0, band), col
+
+    own_at = [spot(offs[0, j], offs[1, j], me) for j in range(count)]
+    above_at = [spot(near[0, 0, j], near[0, 1, j], up) for j in range(count)]
+    below_at = [spot(near[1, 0, j], near[1, 1, j], down) for j in range(count)]
+
+    def wide(plane, col):
+        blank = jnp.zeros((plane.shape[0], LANES), jnp.float32)
+        both = jnp.concatenate([plane, blank], axis=1)
+        return pltpu.roll(both, lax.rem(col, LANES), 1)
+
+    lead = max(0, band - half)
+
+    def place(acc, buf, first_row, plane, start, rows, col):
+        shifted = wide(plane, col)
+        where = slice(first_row, first_row + plane.shape[0])
+        buf[tiles - 1, where, :] = shifted[:, :LANES]
+        buf[tiles, where, :] = shifted[:, LANES:]
+        begin = tiles - 1 - col // LANES
+        for t in range(tiles):
+            acc[t, rows, :] = acc[t, rows, :] + buf[begin + t, pl.ds(start, rows.stop - rows.start), :]
+
+    def place_own(acc, plane, j):
+        row, col = own_at[j]
+        place(acc, zo, lead, plane, lead + half - row, slice(0, band), col)
+
+    def place_above(acc, plane, j):
+        row, col = above_at[j]
+        place(acc, za, 0, plane, band - row, slice(0, half), col)
+
+    def place_below(acc, plane, j):
+        row, col = below_at[j]
+        place(acc, zb, band, plane, band - row, slice(band - half, band), col)
+
+    loads[1].wait()
+    p_re, p_im = probe[0], probe[1]
+    power = p_re * p_re + p_im * p_im
+    accw[...] = jnp.ones_like(accw)
+    acci[...] = jnp.zeros_like(acci)
+    accr[...] = jnp.zeros_like(accr)
+    for j in range(count):
+        place_own(accw, power, j)
+        place_above(accw, power[half:], j)
+        place_below(accw, power[:half], j)
+    accw[...] = 1.0 / accw[...]
+    tall = 64
+
+    def ramp(step, carry):
+        top = pl.multiple_of(step * tall, tall)
+        shape = (tall, width)
+        differ = lax.broadcasted_iota(jnp.int32, shape, 1) - (
+            lax.broadcasted_iota(jnp.int32, shape, 0) + top)
+        spread = differ.astype(jnp.float32)
+        odd = -1.0 / (jnp.maximum(spread * spread, 1.0) * (math.pi * math.pi))
+        value = jnp.where((differ & 1) == 1, odd, jnp.where(differ == 0, 0.25, 0.0))
+        rh[pl.ds(top, tall), :], rl[pl.ds(top, tall), :] = halves(value)
+        return carry
+
+    lax.fori_loop(0, width // tall, ramp, 0)
+    for copy in loads[2:9]:
+        copy.wait()
+    chunk = tables.shape[2]
+    per_row = width // chunk
+    zwin = index.shape[1]
+    per_angle = zwin * per_row
+    deep = 16
+    pattern = lax.broadcasted_iota(jnp.int32, (deep, chunk), 0)
+    one, zero = jnp.ones((deep, chunk), jnp.bfloat16), jnp.zeros((deep, chunk), jnp.bfloat16)
+    pattern = pattern.astype(jnp.int16)
+
+    origins = [me_a] + angle_peers
+
+    def build(k, step, carry):
+        a = origins[k]
+        z = step // per_row
+        lanes = pl.ds(pl.multiple_of(lax.rem(step, per_row) * chunk, chunk), chunk)
+        at = jnp.broadcast_to(index[a, pl.ds(z, 1), lanes], (deep, chunk)).astype(jnp.int16)
+        for r in range(width // deep):
+            hit = at == pattern + jnp.int16(r * deep)
+            tables[k * per_angle + step, r * deep:(r + 1) * deep, :] = jnp.where(hit, one, zero)
+        return carry
+
+    def build_all(k):
+        lax.fori_loop(0, per_angle, functools.partial(build, k), 0)
+
+    for k in range(n_ang):
+        build_all(k)
+    n_re = jnp.zeros((patch, patch), jnp.float32)
+    n_im = n_re
+    den = n_re
+    second, outward, forward = [], [], []
+    for g, group in enumerate(groups):
+        for copy in first[g]:
+            copy.wait()
+        q_re, q_im, w_re, w_im = [], [], [], []
+        for j in group:
+            rows = pl.ds(own_at[j][0], patch)
+            re, im = ext[g][j % size, 0, rows, :], ext[g][j % size, 1, rows, :]
+            q_re.append(re)
+            q_im.append(im)
+            w_re.append(p_re * re - p_im * im)
+            w_im.append(p_re * im + p_im * re)
+        psi = jnp.concatenate([jnp.concatenate(w_re, axis=1), jnp.concatenate(w_im, axis=1)], axis=0)
+        mid = left3(ah[...], al[...], psi)
+        cells = [slice(n * patch, (n + 1) * patch) for n in range(size)]
+        rows = [jnp.concatenate([mid[:patch, cell], mid[patch:, cell]], axis=1) for cell in cells]
+        spec = right3(jnp.concatenate(rows, axis=0), bh[...], bl[...])
+        fixed = []
+        for j, cell in zip(group, cells):
+            s_re = spec[cell, :patch]
+            s_im = spec[cell, patch:]
+            factor = amp[0, j] / jnp.maximum(jnp.sqrt(s_re * s_re + s_im * s_im), 0.5)
+            fixed.append(jnp.concatenate([factor * s_re, factor * s_im], axis=1))
+        back = right3(jnp.concatenate(fixed, axis=0), ah[...], al[...])
+        wide_re = jnp.concatenate([back[cell, :patch] for cell in cells], axis=1)
+        wide_im = jnp.concatenate([back[cell, patch:] for cell in cells], axis=1)
+        diff = left3(bh[...], bl[...], jnp.concatenate([wide_re, wide_im], axis=0))
+        diff = diff - psi
+        for n, j in enumerate(group):
+            d_re, d_im = diff[:patch, cells[n]], diff[patch:, cells[n]]
+            g_re = p_re * d_re + p_im * d_im
+            g_im = p_re * d_im - p_im * d_re
+            twice[n, :patch] = g_im
+            twice[n, patch:] = g_im
+            blk[j] = twice[n, pl.ds(lax.rem(2 * band - (offs[0, j] - me * band), band), band), :]
+            for h in range(2):
+                grad[h, j, 0] = g_re[h * half:(h + 1) * half]
+                grad[h, j, 1] = g_im[h * half:(h + 1) * half]
+            n_re = n_re + (q_re[n] * d_re + q_im[n] * d_im)
+            n_im = n_im + (q_re[n] * d_im - q_im[n] * d_re)
+            den = den + (q_re[n] * q_re[n] + q_im[n] * q_im[n])
+        span = pl.ds(g * size, size)
+        out = [remote(blk.at[span, pl.ds(pl.multiple_of(peer * ns, 8), ns), :], rx.at[n, span],
+                      z_send.at[n, g], z_recv.at[n, g], "angle", peer)
+               for n, peer in enumerate(angle_peers)]
+        mine = remote(blk.at[span, pl.ds(pl.multiple_of(me_a * ns, 8), ns), :], nrx.at[0, span],
+                      f_send.at[0, g], f_recv.at[0, g], "pos", ahead)
+        for copy in out + [mine]:
+            copy.start()
+        outward.append(out)
+        forward.append([mine])
+        pairs = []
+        for c in (1, 0):
+            k = 4 + 6 * g + 2 * (1 - c)
+            pairs.append([
+                remote(grad.at[1, span, c], from_above.at[span, c], send_sem.at[k], recv_sem.at[k], "pos", down),
+                remote(grad.at[0, span, c], from_below.at[span, c], send_sem.at[k + 1], recv_sem.at[k + 1], "pos", up),
+            ])
+        for copy in pairs[0] + ([] if g == len(groups) - 1 else pairs[1]):
+            copy.start()
+        second.append(pairs)
+    numden[0] = n_re
+    numden[1] = n_im
+    numden[2] = den
+    pr = patch // n_pos
+    scatter = [
+        remote(numden.at[:, pl.ds(pl.multiple_of(peer * pr, 8), pr), :], rs.at[d],
+               rs_send.at[d], rs_recv.at[d], "pos", peer)
+        for d, peer in enumerate(pos_peers)
+    ]
+    for copy in scatter:
+        copy.start()
+
+    def whole_patch(j, c):
+        return jnp.concatenate([grad[0, j, c], grad[1, j, c]], axis=0)
+
+    places = [offs] + [far.at[n] for n in range(n_ang - 1)]
+    behinds = [near.at[side]] + [farn.at[n] for n in range(n_ang - 1)]
+    slot = lax.broadcasted_iota(jnp.int32, (ns, LANES), 0) + me_a * ns
+
+    def mark(row, beside):
+        if beside:
+            return jnp.where(side == 0, (slot < row).astype(jnp.float32), (slot >= row + band).astype(jnp.float32))
+        return ((slot >= row) & (slot < row + band)).astype(jnp.float32)
+
+    def lay(acc, n, plane, col):
+        shifted = wide(plane, col)
+        zq[tiles - 1] = shifted[:, :LANES]
+        zq[tiles] = shifted[:, LANES:]
+        begin = tiles - 1 - col // LANES
+        for t in range(tiles):
+            acc[n, t] = acc[n, t] + zq[begin + t]
+
+    def edge(n, j, beside):
+        if beside:
+            return behinds[n][0, j] - behind * band, behinds[n][1, j]
+        return places[n][0, j] - me * band, places[n][1, j]
+
+    for copy in relay:
+        copy.wait()
+    twice[0, :patch] = power
+    twice[0, patch:] = power
+    for n in range(n_ang):
+        for beside in (False, True):
+            for j in range(count):
+                row, col = edge(n, j, beside)
+                begin = lax.rem(me_a * ns + 2 * band - jnp.clip(row, -band, band), band)
+                lay(lw, n, twice[0, pl.ds(begin, ns), :] * mark(row, beside), col)
+    lw[...] = 1.0 / lw[...]
+
+    for j in range(count):
+        place_own(acci, whole_patch(j, 1), j)
+
+    def pass_on(g, n):
+        outward[g][n].wait()
+        copy = remote(rx.at[n, pl.ds(g * size, size)], nrx.at[n + 1, pl.ds(g * size, size)],
+                      f_send.at[n + 1, g], f_recv.at[n + 1, g], "pos", ahead)
+        copy.start()
+        forward[g].append(copy)
+
+    for n in range(n_ang - 1):
+        pass_on(0, n)
+    for copy in second[-1][1]:
+        copy.start()
+    for j in range(count):
+        place_own(accr, whole_patch(j, 0), j)
+    for copy in scatter:
+        copy.wait()
+    part = numden[:, pl.ds(pl.multiple_of(me * pr, 8), pr), :]
+    for d in range(n_pos - 1):
+        part = part + rs[d]
+    partial[...] = part
+    ag[me_a] = part
+    gather = [remote(partial, ag.at[me_a], ag_send.at[n], ag_recv.at[n], "angle", peer)
+              for n, peer in enumerate(angle_peers)]
+    for copy in gather:
+        copy.start()
+
+    def project(k, a, lines):
+        high, low = halves(lines)
+        both = mm(jnp.concatenate([high, low], axis=0), rh[...])
+        lines = (both[:ns] + both[ns:] + mm(high, rl[...])) * (math.pi / n_ang)
+        high, low = halves(lines)
+        next_high, next_low = halves(pltpu.roll(lines, width - 1, 1))
+        stack = jnp.concatenate([high, low, next_high, next_low], axis=0)
+        for n in range(per_angle):
+            z, part = n // per_row, n % per_row
+            got = mm(stack, tables[k * per_angle + n])
+            lower = got[:ns] + got[ns:2 * ns]
+            upper = got[2 * ns:3 * ns] + got[3 * ns:]
+            w = weight[pl.ds(a, 1), z, pl.ds(part * chunk, chunk)]
+            value = (1.0 - w) * lower + w * upper
+            lanes = pl.ds(n * chunk, chunk)
+            recon[:, lanes] = value if k == 0 else recon[:, lanes] + value
+
+    def lines_of(n):
+        for g, group in enumerate(groups):
+            forward[g][n].wait()
+            for j in group:
+                row, col = edge(n, j, False)
+                own = blk[j, pl.ds(pl.multiple_of(me_a * ns, 8), ns), :] if n == 0 else rx[n - 1, j]
+                lay(lg, n, own * mark(row, False), col)
+                row, col = edge(n, j, True)
+                lay(lg, n, nrx[n, j] * mark(row, True), col)
+        rows = pl.ds(pl.multiple_of(me_a * ns, 8), ns)
+        if n > 0:
+            early[n - 1].wait()
+        parts = []
+        for t in range(tiles):
+            base = obj[1, t, rows, :] if n == 0 else orx[n - 1, t]
+            parts.append(base + lg[n, t] * lw[n, t])
+        project(n, origins[n], jnp.concatenate(parts, axis=1))
+
+    pass_on(1, 0) if len(groups) > 1 else None
+    lines_of(0)
+    for g in range(1, len(groups)):
+        for n in range(1 if g == 1 else 0, n_ang - 1):
+            pass_on(g, n)
+    for g, group in enumerate(groups):
+        for copy in second[g][0]:
+            copy.wait()
+        for j in group:
+            place_above(acci, from_above[j, 1], j)
+            place_below(acci, from_below[j, 1], j)
+    for t in range(tiles):
+        lanes = slice(t * LANES, (t + 1) * LANES)
+        newobj[0, 1, :, lanes] = obj[1, t] + acci[t] * accw[t]
+    for copy in gather:
+        copy.wait()
+    total = ag[0]
+    for a in range(1, n_ang):
+        total = total + ag[a]
+    mine = pl.ds(pl.multiple_of(me * pr, 8), pr)
+    for c in range(2):
+        value = total[c] / (total[2] + 1.0)
+        piece[c] = value
+        change[c, mine, :] = value
+    spread = [
+        remote(piece, change.at[:, mine, :], fin_send.at[d], fin_recv.at[d], "pos", peer)
+        for d, peer in enumerate(pos_peers)
+    ]
+    for copy in spread:
+        copy.start()
+    lines_of(1)
+    for g, group in enumerate(groups):
+        for copy in second[g][1]:
+            copy.wait()
+        for j in group:
+            place_above(accr, from_above[j, 0], j)
+            place_below(accr, from_below[j, 0], j)
+    for t in range(tiles):
+        lanes = slice(t * LANES, (t + 1) * LANES)
+        newobj[0, 0, :, lanes] = obj[0, t] + accr[t] * accw[t]
+    for n in range(2, n_ang):
+        lines_of(n)
+    for copy in spread:
+        copy.wait()
+
+
 def tail_kernel(newobj, recon, change, probe, out_obj, out_probe, out_recon, sem):
     copy = pltpu.make_async_copy(newobj, out_obj, sem.at[0])
     copy.start()
@@ -426,29 +829,51 @@
     half_shape = (count, 2, half, patch)
     bits = (n_ang - 1).bit_length()
     links = 2 + 6 * (count // size)
+    base = [
+        VMEM((2, tiles, band, LANES), f32), VMEM(amplitude.shape, f32), VMEM(probe_field.shape, f32),
+        VMEM(interp_index.shape, i32), VMEM(interp_weight.shape, f32), table, table, table, table,
+        [VMEM((size, 2, band + patch, patch), f32)] * (count // size), VMEM((2,) + half_shape, f32),
+        VMEM((ext, lead + half + band, LANES), f32),
+        VMEM((ext, half + band, LANES), f32), VMEM((ext, half + band, LANES), f32),
+    ]
+    sums = [
+        VMEM((tiles, band, LANES), f32), VMEM((tiles, band, LANES), f32), VMEM((tiles, band, LANES), f32),
+        VMEM((2,) + half_shape, f32), VMEM(half_shape, f32), VMEM(half_shape, f32),
+    ]
+    parts = [VMEM((3, patch, patch), f32), VMEM((n_pos - 1, 3, pr, patch), f32)]
+    filters = [VMEM((tables, width, chunk), bf16), VMEM((width, width), bf16), VMEM((width, width), bf16)]
+    groups, peers = count // size, n_ang - 1
+    sems = [dma((9 + tiles,)), dma((links,)), dma((links,)), dma((n_pos - 1,)), dma((n_pos - 1,))]
+    ends = [dma((n_pos - 1,)), dma((n_pos - 1,))]
+    lines = VMEM((n_ang, tiles, ns, LANES), f32)
+    offsets_of = pltpu.SMEM((2, count), i32)
+    if band == patch:
+        kernel = slice_kernel
+        scratch = [
+            offsets_of, pltpu.SMEM((2, 2, count), i32), pltpu.SMEM((peers, 2, count), i32),
+            pltpu.SMEM((peers, 2, count), i32), *base, VMEM((ext, ns, LANES), f32), *sums,
+            VMEM((size, 2 * patch, patch), f32), VMEM((count, band, patch), f32),
+            VMEM((peers, tiles, ns, LANES), f32), VMEM((peers, count, ns, LANES), f32),
+            VMEM((n_ang, count, ns, LANES), f32), lines, lines, *parts,
+            VMEM((3, pr, patch), f32), VMEM((n_ang, 3, pr, patch), f32), VMEM((2, pr, patch), f32), *filters,
+            *sems, dma((peers,)), dma((peers,)), dma((peers,)), dma((peers,)), dma((peers,)), dma((peers,)),
+            dma((peers, groups)), dma((peers, groups)), dma((n_ang, groups)), dma((n_ang, groups)),
+            dma((peers,)), dma((peers,)), *ends,
+        ]
+    else:
+        kernel = step_kernel
+        scratch = [
+            offsets_of, pltpu.SMEM((2, 2, count), i32), *base, *sums, *parts,
+            VMEM((bits, 3, pr, patch), f32), VMEM((bits, 3, pr, patch), f32), VMEM((2, pr, patch), f32),
+            VMEM((peers, ns, width), f32), *filters, *sems,
+            dma((peers,)), dma((peers,)), dma((bits,)), dma((bits,)), *ends,
+        ]
     newobj, recon, change = pl.pallas_call(
-        functools.partial(step_kernel, n_ang, n_pos, size),
+        functools.partial(kernel, n_ang, n_pos, size),
         out_shape=(VMEM(object_field.shape, f32), VMEM((ns, total), f32), VMEM(probe_field.shape, f32)),
         in_specs=[hbm] * 10,
         out_specs=(vmem,) * 3,
-        scratch_shapes=[
-            pltpu.SMEM((2, count), i32), pltpu.SMEM((2, 2, count), i32),
-            VMEM((2, tiles, band, LANES), f32), VMEM(amplitude.shape, f32), VMEM(probe_field.shape, f32),
-            VMEM(interp_index.shape, i32), VMEM(interp_weight.shape, f32),
-            table, table, table, table,
-            [VMEM((size, 2, band + patch, patch), f32)] * (count // size), VMEM((2,) + half_shape, f32),
-            VMEM((ext, lead + half + band, LANES), f32),
-            VMEM((ext, half + band, LANES), f32), VMEM((ext, half + band, LANES), f32),
-            VMEM((tiles, band, LANES), f32), VMEM((tiles, band, LANES), f32), VMEM((tiles, band, LANES), f32),
-            VMEM((2,) + half_shape, f32), VMEM(half_shape, f32), VMEM(half_shape, f32),
-            VMEM((3, patch, patch), f32), VMEM((n_pos - 1, 3, pr, patch), f32),
-            VMEM((bits, 3, pr, patch), f32), VMEM((bits, 3, pr, patch), f32), VMEM((2, pr, patch), f32),
-            VMEM((n_ang - 1, ns, width), f32),
-            VMEM((tables, width, chunk), bf16), VMEM((width, width), bf16), VMEM((width, width), bf16),
-            dma((9 + tiles,)), dma((links,)), dma((links,)), dma((n_pos - 1,)), dma((n_pos - 1,)),
-            dma((n_ang - 1,)), dma((n_ang - 1,)), dma((bits,)), dma((bits,)),
-            dma((n_pos - 1,)), dma((n_pos - 1,)),
-        ],
+        scratch_shapes=scratch,
         compiler_params=pltpu.CompilerParams(
             collective_id=0, has_side_effects=True, vmem_limit_bytes=KLIMIT),
         name="step",

time: 42.3 us -> 38.8 us (0.917)
  Pallas kernels: 41.5 us -> 38 us
    pallas_call x1, Pallas kernels: 39.8 us -> 36.2 us  [on_device(): pl.pallas_call(functools.partial(kernel, n_ang, n_pos, size), out_shape=(...]
where the time goes in v3:
time: 38.8 us; the launch traced here: 38.6 us
  Pallas kernels  38 us (98%)
  between operations  0.66 us (2%)
    pallas_call x1, Pallas kernels, on_device(): pl.pallas_call(functools.partial(kernel, n_ang, n_pos, size), out_shape=(...  36.2 us
    pallas_call x1, Pallas kernels, on_device(): pl.pallas_call(tail_kernel, out_shape=(sds(object_field.shape, f32), sds(...  1.73 us

profile of v3, /device:TPU:0, one launch (start us, length us, event | category | flops | bytes accessed | tf_op | source)
XLA Modules:
  0.0 38.6 jit_solution(18295207534738811162)
XLA Ops:
  0.6 0.0 copy-start
  0.6 36.2 %step.1 = (f32[1,2,128,1024]{3,2,1,0:T(8,128)S(1)}, f32[32,2048]{1,0:T(8,128)S(1)}, f32[2,128,128]{2,1,0:T(8,128)S(1)}) custom-call(s32[2,4]{1,0:T(2,128)} %bitcast.3, f32[1,2,128,1024]{3,2,1,0:T(8,128)} %obj_h.1, f32[1,4,128,128]{3,2,1,0:T(8,128)} %amp_h.1, f32[2,128,128]{2,1,0:T(8,128)} %probe.1, s32[4,2,1024]{2,1,0:T(2,128)} %index_h.1, ...), custom_call_target="tpu_custom_call" | custom-call | tf_op jit(solution)/shard_map/step/pallas_call | solution.py:871
  36.9 0.0 copy-done
  36.9 1.7 %tail.1 = (f32[1,2,128,1024]{3,2,1,0:T(8,128)}, f32[2,128,128]{2,1,0:T(8,128)}, f32[1,32,2,1024]{3,2,1,0:T(2,128)}) custom-call(f32[1,2,128,1024]{3,2,1,0:T(8,128)S(1)} %get-tuple-element.6.newobj, f32[32,2048]{1,0:T(8,128)S(1)} %get-tuple-element.7.recon, f32[2,128,128]{2,1,0:T(8,128)S(1)} %get-tuple-element.8.change, f32[2,128,128]{2,1,0:T(8,128)S(1)} %copy-done), custom_call_target="tpu_custom_call" | custom-call | tf_op jit(solution)/shard_map/tail/pallas_call | solution.py:883
Async XLA Ops:
  0.6 36.2 %copy-start = (f32[2,128,128]{2,1,0:T(8,128)S(1)}, f32[2,128,128]{2,1,0:T(8,128)}, u32[]{:S(2)}) copy-start(f32[2,128,128]{2,1,0:T(8,128)} %probe.1) | copy-start | bytes 393220

commit v4 on v3

--- a/solution.py
+++ b/solution.py
@@ -393,8 +393,8 @@
                  offs, near, far, farn, obj, amp, probe, index, weight, ah, al, bh, bl,
                  ext, sb, zo, za, zb, zq, accw, acci, accr, grad, from_above, from_below,
                  twice, blk, orx, rx, nrx, lw, lg,
-                 numden, rs, partial, ag, piece, tables, rh, rl,
-                 in_sem, send_sem, recv_sem, rs_send, rs_recv, far_send, far_recv, farn_send, farn_recv,
+                 numden, rs, paired, partial, ag, piece, tables, rh, rl,
+                 in_sem, send_sem, recv_sem, rs_send, rs_recv, pair_sem, far_send, far_recv, farn_send, farn_recv,
                  o_send, o_recv, z_send, z_recv, f_send, f_recv, ag_send, ag_recv, fin_send, fin_recv):
     me_a = lax.axis_index("angle")
     me = lax.axis_index("pos")
@@ -457,6 +457,11 @@
     lw[...] = jnp.ones_like(lw)
     for k, copy in enumerate(swap):
         copy.wait()
+    relay = [remote(far.at[n], farn.at[n], farn_send.at[n], farn_recv.at[n], "pos", ahead)
+             for n in range(n_ang - 1)]
+    for n in range(n_ang - 1):
+        reach[n].wait()
+        relay[n].start()
     first = []
     groups = [range(g * size, (g + 1) * size) for g in range(count // size)]
     for g, group in enumerate(groups):
@@ -474,11 +479,6 @@
         for copy in pair:
             copy.start()
         first.append(pair)
-    relay = [remote(far.at[n], farn.at[n], farn_send.at[n], farn_recv.at[n], "pos", ahead)
-             for n in range(n_ang - 1)]
-    for n in range(n_ang - 1):
-        reach[n].wait()
-        relay[n].start()
 
     def spot(row, col, owner):
         return jnp.clip(row - owner * band + half, 0, band), col
@@ -568,6 +568,40 @@
 
     for k in range(n_ang):
         build_all(k)
+    places = [offs] + [far.at[n] for n in range(n_ang - 1)]
+    behinds = [near.at[side]] + [farn.at[n] for n in range(n_ang - 1)]
+    slot = lax.broadcasted_iota(jnp.int32, (ns, LANES), 0) + me_a * ns
+
+    def mark(row, beside):
+        if beside:
+            return jnp.where(side == 0, (slot < row).astype(jnp.float32), (slot >= row + band).astype(jnp.float32))
+        return ((slot >= row) & (slot < row + band)).astype(jnp.float32)
+
+    def lay(acc, n, plane, col):
+        shifted = wide(plane, col)
+        zq[tiles - 1] = shifted[:, :LANES]
+        zq[tiles] = shifted[:, LANES:]
+        begin = tiles - 1 - col // LANES
+        for t in range(tiles):
+            acc[n, t] = acc[n, t] + zq[begin + t]
+
+    def edge(n, j, beside):
+        if beside:
+            return behinds[n][0, j] - behind * band, behinds[n][1, j]
+        return places[n][0, j] - me * band, places[n][1, j]
+
+    for copy in relay:
+        copy.wait()
+    twice[0, :patch] = power
+    twice[0, patch:] = power
+    for n in range(n_ang):
+        for beside in (False, True):
+            for j in range(count):
+                row, col = edge(n, j, beside)
+                begin = lax.rem(me_a * ns + 2 * band - jnp.clip(row, -band, band), band)
+                lay(lw, n, twice[0, pl.ds(begin, ns), :] * mark(row, beside), col)
+    lw[...] = 1.0 / lw[...]
+
     n_re = jnp.zeros((patch, patch), jnp.float32)
     n_im = n_re
     den = n_re
@@ -636,53 +670,26 @@
     numden[1] = n_im
     numden[2] = den
     pr = patch // n_pos
+    core, chip, chips = me % 2, me // 2, n_pos // 2
+    swap_half = remote(numden.at[:, pl.ds(pl.multiple_of((1 - core) * half, 8), half), :], paired.at[0],
+                       pair_sem.at[0], pair_sem.at[1], "pos", me + 1 - 2 * core)
+    swap_half.start()
+
+    def whole_patch(j, c):
+        return jnp.concatenate([grad[0, j, c], grad[1, j, c]], axis=0)
+
+    for j in range(count):
+        place_own(acci, whole_patch(j, 1), j)
+    swap_half.wait()
+    paired[1] = paired[0] + numden[:, pl.ds(pl.multiple_of(core * half, 8), half), :]
+    chip_peers = [lax.rem(chip + d, chips) for d in range(1, chips)]
     scatter = [
-        remote(numden.at[:, pl.ds(pl.multiple_of(peer * pr, 8), pr), :], rs.at[d],
-               rs_send.at[d], rs_recv.at[d], "pos", peer)
-        for d, peer in enumerate(pos_peers)
+        remote(paired.at[1, :, pl.ds(pl.multiple_of(peer * pr, 8), pr), :], rs.at[d],
+               rs_send.at[d], rs_recv.at[d], "pos", 2 * peer + core)
+        for d, peer in enumerate(chip_peers)
     ]
     for copy in scatter:
         copy.start()
-
-    def whole_patch(j, c):
-        return jnp.concatenate([grad[0, j, c], grad[1, j, c]], axis=0)
-
-    places = [offs] + [far.at[n] for n in range(n_ang - 1)]
-    behinds = [near.at[side]] + [farn.at[n] for n in range(n_ang - 1)]
-    slot = lax.broadcasted_iota(jnp.int32, (ns, LANES), 0) + me_a * ns
-
-    def mark(row, beside):
-        if beside:
-            return jnp.where(side == 0, (slot < row).astype(jnp.float32), (slot >= row + band).astype(jnp.float32))
-        return ((slot >= row) & (slot < row + band)).astype(jnp.float32)
-
-    def lay(acc, n, plane, col):
-        shifted = wide(plane, col)
-        zq[tiles - 1] = shifted[:, :LANES]
-        zq[tiles] = shifted[:, LANES:]
-        begin = tiles - 1 - col // LANES
-        for t in range(tiles):
-            acc[n, t] = acc[n, t] + zq[begin + t]
-
-    def edge(n, j, beside):
-        if beside:
-            return behinds[n][0, j] - behind * band, behinds[n][1, j]
-        return places[n][0, j] - me * band, places[n][1, j]
-
-    for copy in relay:
-        copy.wait()
-    twice[0, :patch] = power
-    twice[0, patch:] = power
-    for n in range(n_ang):
-        for beside in (False, True):
-            for j in range(count):
-                row, col = edge(n, j, beside)
-                begin = lax.rem(me_a * ns + 2 * band - jnp.clip(row, -band, band), band)
-                lay(lw, n, twice[0, pl.ds(begin, ns), :] * mark(row, beside), col)
-    lw[...] = 1.0 / lw[...]
-
-    for j in range(count):
-        place_own(acci, whole_patch(j, 1), j)
 
     def pass_on(g, n):
         outward[g][n].wait()
@@ -691,64 +698,90 @@
         copy.start()
         forward[g].append(copy)
 
-    for n in range(n_ang - 1):
-        pass_on(0, n)
-    for copy in second[-1][1]:
-        copy.start()
-    for j in range(count):
-        place_own(accr, whole_patch(j, 0), j)
-    for copy in scatter:
-        copy.wait()
-    part = numden[:, pl.ds(pl.multiple_of(me * pr, 8), pr), :]
-    for d in range(n_pos - 1):
-        part = part + rs[d]
-    partial[...] = part
-    ag[me_a] = part
     gather = [remote(partial, ag.at[me_a], ag_send.at[n], ag_recv.at[n], "angle", peer)
               for n, peer in enumerate(angle_peers)]
-    for copy in gather:
-        copy.start()
-
-    def project(k, a, lines):
-        high, low = halves(lines)
-        both = mm(jnp.concatenate([high, low], axis=0), rh[...])
-        lines = (both[:ns] + both[ns:] + mm(high, rl[...])) * (math.pi / n_ang)
+
+    def share():
+        for copy in scatter:
+            copy.wait()
+        part = paired[1, :, pl.ds(pl.multiple_of(chip * pr, 8), pr), :]
+        for d in range(chips - 1):
+            part = part + rs[d]
+        partial[...] = part
+        ag[me_a] = part
+        for copy in gather:
+            copy.start()
+
+    origins_of = [me_a] + angle_peers
+    here = pl.ds(pl.multiple_of(me_a * ns, 8), ns)
+
+    def lay_own(g, n):
+        for j in groups[g]:
+            row, col = edge(n, j, False)
+            own = blk[j, here, :] if n == 0 else rx[n - 1, j]
+            lay(lg, n, own * mark(row, False), col)
+
+    def lay_beside(g, n):
+        forward[g][n].wait()
+        for j in groups[g]:
+            row, col = edge(n, j, True)
+            lay(lg, n, nrx[n, j] * mark(row, True), col)
+
+    def filtered(ns_of):
+        tops, lows = [], []
+        for n in ns_of:
+            parts = []
+            for t in range(tiles):
+                base = obj[1, t, here, :] if n == 0 else orx[n - 1, t]
+                parts.append(base + lg[n, t] * lw[n, t])
+            high, low = halves(jnp.concatenate(parts, axis=1))
+            tops.append(high)
+            lows.append(low)
+        both = mm(jnp.concatenate(tops + lows, axis=0), rh[...])
+        more = mm(jnp.concatenate(tops, axis=0), rl[...])
+        size_of = len(ns_of) * ns
+        total = (both[:size_of] + both[size_of:] + more) * (math.pi / n_ang)
+        return [total[m * ns:(m + 1) * ns] for m in range(len(ns_of))]
+
+    def spread_out(n, lines):
+        a = origins_of[n]
         high, low = halves(lines)
         next_high, next_low = halves(pltpu.roll(lines, width - 1, 1))
         stack = jnp.concatenate([high, low, next_high, next_low], axis=0)
-        for n in range(per_angle):
-            z, part = n // per_row, n % per_row
-            got = mm(stack, tables[k * per_angle + n])
+        for m in range(per_angle):
+            z, part = m // per_row, m % per_row
+            got = mm(stack, tables[n * per_angle + m])
             lower = got[:ns] + got[ns:2 * ns]
             upper = got[2 * ns:3 * ns] + got[3 * ns:]
             w = weight[pl.ds(a, 1), z, pl.ds(part * chunk, chunk)]
             value = (1.0 - w) * lower + w * upper
-            lanes = pl.ds(n * chunk, chunk)
-            recon[:, lanes] = value if k == 0 else recon[:, lanes] + value
-
-    def lines_of(n):
-        for g, group in enumerate(groups):
-            forward[g][n].wait()
-            for j in group:
-                row, col = edge(n, j, False)
-                own = blk[j, pl.ds(pl.multiple_of(me_a * ns, 8), ns), :] if n == 0 else rx[n - 1, j]
-                lay(lg, n, own * mark(row, False), col)
-                row, col = edge(n, j, True)
-                lay(lg, n, nrx[n, j] * mark(row, True), col)
-        rows = pl.ds(pl.multiple_of(me_a * ns, 8), ns)
-        if n > 0:
-            early[n - 1].wait()
-        parts = []
-        for t in range(tiles):
-            base = obj[1, t, rows, :] if n == 0 else orx[n - 1, t]
-            parts.append(base + lg[n, t] * lw[n, t])
-        project(n, origins[n], jnp.concatenate(parts, axis=1))
-
-    pass_on(1, 0) if len(groups) > 1 else None
-    lines_of(0)
-    for g in range(1, len(groups)):
-        for n in range(1 if g == 1 else 0, n_ang - 1):
+            lanes = pl.ds(m * chunk, chunk)
+            recon[:, lanes] = value if n == 0 else recon[:, lanes] + value
+
+    def whole_lines(ns_of):
+        for n, lines in zip(ns_of, filtered(ns_of)):
+            spread_out(n, lines)
+
+    later = range(1, len(groups))
+    for j in range(count):
+        place_own(accr, whole_patch(j, 0), j)
+    for n in range(n_ang - 1):
+        pass_on(0, n)
+        lay_own(0, n + 1)
+    for g in range(len(groups)):
+        lay_own(g, 0)
+        lay_beside(g, 0)
+    whole_lines([0])
+    for g in later:
+        for n in range(n_ang - 1):
             pass_on(g, n)
+            if n == 0:
+                share()
+            lay_own(g, n + 1)
+    if len(groups) == 1:
+        share()
+    for copy in second[-1][1]:
+        copy.start()
     for g, group in enumerate(groups):
         for copy in second[g][0]:
             copy.wait()
@@ -758,12 +791,17 @@
     for t in range(tiles):
         lanes = slice(t * LANES, (t + 1) * LANES)
         newobj[0, 1, :, lanes] = obj[1, t] + acci[t] * accw[t]
+    for copy in early:
+        copy.wait()
+    for g in range(len(groups)):
+        lay_beside(g, 1)
+    whole_lines([1])
     for copy in gather:
         copy.wait()
     total = ag[0]
     for a in range(1, n_ang):
         total = total + ag[a]
-    mine = pl.ds(pl.multiple_of(me * pr, 8), pr)
+    mine = pl.ds(pl.multiple_of(core * half + chip * pr, 8), pr)
     for c in range(2):
         value = total[c] / (total[2] + 1.0)
         piece[c] = value
@@ -774,7 +812,11 @@
     ]
     for copy in spread:
         copy.start()
-    lines_of(1)
+    for n in range(2, n_ang):
+        for g in range(len(groups)):
+            lay_beside(g, n)
+    if n_ang > 2:
+        whole_lines(list(range(2, n_ang)))
     for g, group in enumerate(groups):
         for copy in second[g][1]:
             copy.wait()
@@ -784,8 +826,6 @@
     for t in range(tiles):
         lanes = slice(t * LANES, (t + 1) * LANES)
         newobj[0, 0, :, lanes] = obj[0, t] + accr[t] * accw[t]
-    for n in range(2, n_ang):
-        lines_of(n)
     for copy in spread:
         copy.wait()
 
@@ -854,9 +894,9 @@
             pltpu.SMEM((peers, 2, count), i32), *base, VMEM((ext, ns, LANES), f32), *sums,
             VMEM((size, 2 * patch, patch), f32), VMEM((count, band, patch), f32),
             VMEM((peers, tiles, ns, LANES), f32), VMEM((peers, count, ns, LANES), f32),
-            VMEM((n_ang, count, ns, LANES), f32), lines, lines, *parts,
+            VMEM((n_ang, count, ns, LANES), f32), lines, lines, *parts, VMEM((2, 3, half, patch), f32),
             VMEM((3, pr, patch), f32), VMEM((n_ang, 3, pr, patch), f32), VMEM((2, pr, patch), f32), *filters,
-            *sems, dma((peers,)), dma((peers,)), dma((peers,)), dma((peers,)), dma((peers,)), dma((peers,)),
+            *sems, dma((2,)), dma((peers,)), dma((peers,)), dma((peers,)), dma((peers,)), dma((peers,)), dma((peers,)),
             dma((peers, groups)), dma((peers, groups)), dma((n_ang, groups)), dma((n_ang, groups)),
             dma((peers,)), dma((peers,)), *ends,
         ]

time: 38.8 us -> 36.1 us (0.930)
  Pallas kernels: 38 us -> 35.3 us
    pallas_call x1, Pallas kernels: 36.2 us -> 33.5 us  [on_device(): pl.pallas_call(functools.partial(kernel, n_ang, n_pos, size), out_shape=(...]
where the time goes in v4:
time: 36.1 us; the launch traced here: 35.9 us
  Pallas kernels  35.3 us (98%)
  between operations  0.66 us (2%)
    pallas_call x1, Pallas kernels, on_device(): pl.pallas_call(functools.partial(kernel, n_ang, n_pos, size), out_shape=(...  33.5 us
    pallas_call x1, Pallas kernels, on_device(): pl.pallas_call(tail_kernel, out_shape=(sds(object_field.shape, f32), sds(...  1.73 us

profile of v4, /device:TPU:0, one launch (start us, length us, event | category | flops | bytes accessed | tf_op | source)
XLA Modules:
  0.0 35.9 jit_solution(14270032307771336891)
XLA Ops:
  0.6 0.0 copy-start
  0.6 33.5 %step.1 = (f32[1,2,128,1024]{3,2,1,0:T(8,128)S(1)}, f32[32,2048]{1,0:T(8,128)S(1)}, f32[2,128,128]{2,1,0:T(8,128)S(1)}) custom-call(s32[2,4]{1,0:T(2,128)} %bitcast.3, f32[1,2,128,1024]{3,2,1,0:T(8,128)} %obj_h.1, f32[1,4,128,128]{3,2,1,0:T(8,128)} %amp_h.1, f32[2,128,128]{2,1,0:T(8,128)} %probe.1, s32[4,2,1024]{2,1,0:T(2,128)} %index_h.1, ...), custom_call_target="tpu_custom_call" | custom-call | tf_op jit(solution)/shard_map/step/pallas_call | solution.py:911
  34.2 0.0 copy-done
  34.2 1.7 %tail.1 = (f32[1,2,128,1024]{3,2,1,0:T(8,128)}, f32[2,128,128]{2,1,0:T(8,128)}, f32[1,32,2,1024]{3,2,1,0:T(2,128)}) custom-call(f32[1,2,128,1024]{3,2,1,0:T(8,128)S(1)} %get-tuple-element.6.newobj, f32[32,2048]{1,0:T(8,128)S(1)} %get-tuple-element.7.recon, f32[2,128,128]{2,1,0:T(8,128)S(1)} %get-tuple-element.8.change, f32[2,128,128]{2,1,0:T(8,128)S(1)} %copy-done), custom_call_target="tpu_custom_call" | custom-call | tf_op jit(solution)/shard_map/tail/pallas_call | solution.py:923
Async XLA Ops:
  0.6 33.6 %copy-start = (f32[2,128,128]{2,1,0:T(8,128)S(1)}, f32[2,128,128]{2,1,0:T(8,128)}, u32[]{:S(2)}) copy-start(f32[2,128,128]{2,1,0:T(8,128)} %probe.1) | copy-start | bytes 393220

commit v5 on v4

--- a/solution.py
+++ b/solution.py
@@ -413,8 +413,6 @@
                (ah_h, ah), (al_h, al), (bh_h, bh), (bl_h, bl), (index_h, index), (weight_h, weight)]
     sources += [(obj_h.at[0, :, :, pl.ds(t * LANES, LANES)], obj.at[:, t]) for t in range(tiles)]
     loads = [pltpu.make_async_copy(src, dst, in_sem.at[k]) for k, (src, dst) in enumerate(sources)]
-    for copy in loads:
-        copy.start()
     bits = (n_ang - 1).bit_length()
     order = [1] + list(range(n_ang - 1, 1, -1))
     angle_peers = [flip(me_a, mask, bits) for mask in order]
@@ -424,6 +422,8 @@
         pl.semaphore_signal(barrier, inc=1, device_id={"pos": peer}, device_id_type=MESH)
     for peer in angle_peers:
         pl.semaphore_signal(barrier, inc=1, device_id={"angle": peer}, device_id_type=MESH)
+    for copy in loads:
+        copy.start()
     loads[0].wait()
     pl.semaphore_wait(barrier, n_ang + n_pos - 2)
     swap = [remote(offs, near.at[0], send_sem.at[0], recv_sem.at[0], "pos", down),
@@ -772,14 +772,11 @@
         lay_own(g, 0)
         lay_beside(g, 0)
     whole_lines([0])
+    share()
     for g in later:
         for n in range(n_ang - 1):
             pass_on(g, n)
-            if n == 0:
-                share()
             lay_own(g, n + 1)
-    if len(groups) == 1:
-        share()
     for copy in second[-1][1]:
         copy.start()
     for g, group in enumerate(groups):

time: 36.1 us -> 36 us (level)
  no operation moved by 1% of the time
where the time goes in v5:
time: 36 us; the launch traced here: 35.9 us
  Pallas kernels  35.2 us (98%)
  between operations  0.66 us (2%)
    pallas_call x1, Pallas kernels, on_device(): pl.pallas_call(functools.partial(kernel, n_ang, n_pos, size), out_shape=(...  33.5 us
    pallas_call x1, Pallas kernels, on_device(): pl.pallas_call(tail_kernel, out_shape=(sds(object_field.shape, f32), sds(...  1.73 us

profile of v5, /device:TPU:0, one launch (start us, length us, event | category | flops | bytes accessed | tf_op | source)
XLA Modules:
  0.0 35.9 jit_solution(116933060571961398)
XLA Ops:
  0.6 0.0 copy-start
  0.6 33.5 %step.1 = (f32[1,2,128,1024]{3,2,1,0:T(8,128)S(1)}, f32[32,2048]{1,0:T(8,128)S(1)}, f32[2,128,128]{2,1,0:T(8,128)S(1)}) custom-call(s32[2,4]{1,0:T(2,128)} %bitcast.3, f32[1,2,128,1024]{3,2,1,0:T(8,128)} %obj_h.1, f32[1,4,128,128]{3,2,1,0:T(8,128)} %amp_h.1, f32[2,128,128]{2,1,0:T(8,128)} %probe.1, s32[4,2,1024]{2,1,0:T(2,128)} %index_h.1, ...), custom_call_target="tpu_custom_call" | custom-call | tf_op jit(solution)/shard_map/step/pallas_call | solution.py:908
  34.1 0.0 copy-done
  34.1 1.7 %tail.1 = (f32[1,2,128,1024]{3,2,1,0:T(8,128)}, f32[2,128,128]{2,1,0:T(8,128)}, f32[1,32,2,1024]{3,2,1,0:T(2,128)}) custom-call(f32[1,2,128,1024]{3,2,1,0:T(8,128)S(1)} %get-tuple-element.6.newobj, f32[32,2048]{1,0:T(8,128)S(1)} %get-tuple-element.7.recon, f32[2,128,128]{2,1,0:T(8,128)S(1)} %get-tuple-element.8.change, f32[2,128,128]{2,1,0:T(8,128)S(1)} %copy-done), custom_call_target="tpu_custom_call" | custom-call | tf_op jit(solution)/shard_map/tail/pallas_call | solution.py:920
Async XLA Ops:
  0.6 33.5 %copy-start = (f32[2,128,128]{2,1,0:T(8,128)S(1)}, f32[2,128,128]{2,1,0:T(8,128)}, u32[]{:S(2)}) copy-start(f32[2,128,128]{2,1,0:T(8,128)} %probe.1) | copy-start | bytes 393220
